TPU v7x, 32 devices: a whole 2x2x4 slice. The times are simulated.
32 devices in a mesh: rows: 16 (over z, y, x), inner: 2 (over core).
Axes of the slice: x: 2, y: 2, z: 4, core: 2. Of those that a mesh axis runs over, the one named last changes fastest.
Arguments:
- r_tiles: bfloat16 [128, 16, 128, 128], P('rows', 'inner'), may hold values from -0.5 to 0.5
- r_cols: int32 [128, 16], P('rows', 'inner'), may hold values from 0 to 255, as said below
- a_tiles: bfloat16 [256, 7, 128, 128], P(('rows', 'inner')), may hold values from -6 to 6
- a_cols: int32 [256, 7], replicated, may hold values from 0 to 255, as said below
- c_cols: int32 [128, 8], P('rows'), may hold values from -1 to 255, as said below
- c_counts: int32 [128], P('rows'), may hold values from 4 to 8, as said below
Outputs:
- c_tiles: bfloat16 [128, 8, 128, 128], P('rows', 'inner')
- row_offsets: int32 [128], P('rows')
Inputs may be any that keep to these rules, and one draw needn't show every extreme that they name: `r_cols`: the slots g * 8 to (g + 1) * 8 - 1 of block row c name distinct fine block rows k with (k // 8) % 2 == g and k // 16 within one of c // 8. `a_cols`: row k names 7 distinct fine block columns, the first of them k. `c_cols`: the first c_counts[c] entries of row c are distinct block columns, the others are -1. `c_counts`: each aligned group of 8 block rows has one with 8 live slots.
All inputs are finite; a program needn't handle non-finite values.
Results may differ from a plain program's by a relative error of at most 0.001.
Values may be sent and summed in bfloat16 or wider, within the bound.
A program may use at most 64 MiB of HBM per device.

v0:
```python
import functools

import jax
import jax.numpy as jnp
from jax import lax
from jax.experimental import pallas as pl
from jax.experimental.pallas import tpu as pltpu
from jax.sharding import PartitionSpec as P

MESH = pl.DeviceIdType.MESH
BATCH = 4


def plan_kernel(
    dims, r_cols_ref, c_cols_ref, counts_ref, columns_ref, code_ref, plan_ref,
    meta_ref, gathered, needs, send_sem, recv_sem,
):
    rows, groups, local_rows, op_slots, r_slots, cap, half = dims
    width = 2 * half
    count = rows * groups
    tiles = local_rows * op_slots
    row = lax.axis_index("rows")
    group = lax.axis_index("inner")
    me = row * groups + group

    barrier = pltpu.get_barrier_semaphore()

    def place(step):
        other = lax.rem(me + step, count)
        return (other // groups, lax.rem(other, groups))

    def greet(step, carry):
        pl.semaphore_signal(barrier, inc=1, device_id=place(step), device_id_type=MESH)
        return carry

    lax.fori_loop(1, count, greet, 0)
    row_count = r_cols_ref.shape[0]
    live = r_slots + cap
    lanes = lax.broadcasted_iota(jnp.int32, (row_count, width), 1)
    above = lax.broadcasted_iota(jnp.int32, (row_count, width), 0)
    small = (row_count, row_count)
    diagonal = lax.broadcasted_iota(jnp.int32, small, 0) == lax.broadcasted_iota(jnp.int32, small, 1)
    spread_counts = jnp.broadcast_to(counts_ref[...], small)
    own_counts = jnp.sum(jnp.where(diagonal, spread_counts, 0), axis=1, keepdims=True)
    meta_ref[...] = jnp.full(meta_ref.shape, -9, jnp.int32)
    meta_ref[:, 0:r_slots] = r_cols_ref[...]
    meta_ref[:, r_slots:live] = c_cols_ref[...]
    meta_ref[:, live : live + 1] = own_counts
    gathered[me] = meta_ref[...]
    pl.semaphore_wait(barrier, count - 1)

    def post(step, carry):
        pltpu.make_async_remote_copy(
            src_ref=meta_ref,
            dst_ref=gathered.at[me],
            send_sem=send_sem,
            recv_sem=recv_sem,
            device_id=place(step),
            device_id_type=MESH,
        ).start()
        return carry

    lax.fori_loop(1, count, post, 0)
    everyone = gathered.at[pl.ds(0, count - 1)]
    pltpu.make_async_copy(everyone, everyone, send_sem).wait()
    pltpu.make_async_copy(everyone, everyone, recv_sem).wait()

    def matches(block, columns, fine_rows):
        named = fine_rows == block[:, 0:1]
        for j in range(1, r_slots):
            named = named | (fine_rows == block[:, j : j + 1])
        slot = jnp.full((row_count, width), -1, jnp.int32)
        for s in range(cap):
            slot = jnp.where(columns == block[:, r_slots + s : r_slots + s + 1], s, slot)
        return jnp.where(named, slot, -1)

    shift = jnp.where(lanes < half, -groups, groups) * local_rows
    tile = jnp.where(lanes < half, lanes, lanes - half)
    lane_rows = jnp.where(tile < tiles, shift + tile // op_slots, -(1 << 24))
    low_lanes = lanes[0:1] < half

    def near_matches(device):
        before = columns_ref[pl.ds(jnp.maximum(device - groups, 0), 1), :]
        after = columns_ref[pl.ds(jnp.minimum(device + groups, count - 1), 1), :]
        columns = jnp.where(low_lanes, before, after)
        return matches(gathered[device], columns, lane_rows + device * local_rows)

    def wanted(found):
        return jnp.max((found >= 0).astype(jnp.int32), axis=0, keepdims=True)

    def gather_needs(device, carry):
        needs[pl.ds(device, 1), :] = wanted(near_matches(device))
        return carry

    lax.fori_loop(0, count, gather_needs, 0, unroll=4)
    every = needs[...]
    low_side = lax.broadcasted_iota(jnp.int32, every.shape, 1) < half
    low = jnp.sum(jnp.where(low_side, every, 0), axis=1, keepdims=True)
    high = jnp.sum(jnp.where(low_side, 0, every), axis=1, keepdims=True)
    most = jnp.max(jnp.maximum(low, high), axis=0, keepdims=True)

    down = lax.broadcasted_iota(jnp.int32, (width, width), 0)
    across = lax.broadcasted_iota(jnp.int32, (width, width), 1)
    same = (down < half) == (across < half)

    def ranks(need):
        spread = jnp.broadcast_to(need, (width, width))
        column = jnp.sum(jnp.where(down == across, spread, 0), axis=1, keepdims=True)
        before = jnp.sum(jnp.where((across < down) & same, spread, 0), axis=1, keepdims=True)
        along = jnp.sum(
            jnp.where((down < across) & same, jnp.broadcast_to(column, (width, width)), 0),
            axis=0,
            keepdims=True,
        )
        return column, before, along

    def send_list(device, high):
        column, before, _ = ranks(needs[pl.ds(device, 1), :])
        first = half if high else 0
        mine = (down >= half) if high else (down < half)
        chosen = mine & (column > 0) & (before == across)
        return jnp.sum(jnp.where(chosen, down - first, 0), axis=0, keepdims=True)

    left = jnp.maximum(row - 1, 0) * groups + group
    right = jnp.minimum(row + 1, rows - 1) * groups + group
    plan_ref[0:1, :] = send_list(left, True)
    plan_ref[1:2, :] = send_list(right, False)

    found = near_matches(me)
    _, _, along = ranks(wanted(found))
    slot_at = along + jnp.where(lanes[0:1] < half, tiles, 2 * tiles)
    code_ref[:, 0:width] = jnp.where(found >= 0, found + cap * slot_at, -1)
    fine = me * local_rows + jnp.where(lanes < tiles, lanes // op_slots, 0)
    fine = jnp.where(lanes < tiles, fine, -5)
    found = matches(gathered[me], columns_ref[pl.ds(me, 1), :], fine)
    code_ref[:, width:] = jnp.where(found >= 0, found + cap * lanes, -1)

    def earlier(index, total):
        block = gathered[index * groups]
        return total + jnp.sum(block[:, live : live + 1], axis=0, keepdims=True)

    first = lax.fori_loop(0, row, earlier, jnp.zeros((1, 1), jnp.int32))
    counts = jnp.broadcast_to(own_counts, (row_count, width))
    inner_sum = jnp.sum(jnp.where(above < lanes, counts, 0), axis=0, keepdims=True)
    plan_ref[2:3, :] = inner_sum + first
    level = jnp.zeros((1, 1), jnp.int32)
    for size in sizes_for(tiles)[:-1]:
        level = level + (most > size).astype(jnp.int32)
    plan_ref[3:4, :] = jnp.broadcast_to(level, (1, width))


def halo_kernel(rows, size, plan_ref, a_ref, out_ref, packed, send_sems, recv_sems):
    row = lax.axis_index("rows")
    group = lax.axis_index("inner")
    barrier = pltpu.get_barrier_semaphore()
    has_left = row > 0
    has_right = row < rows - 1

    @pl.when(has_left)
    def _():
        pl.semaphore_signal(barrier, inc=1, device_id=(row - 1, group), device_id_type=MESH)

    @pl.when(has_right)
    def _():
        pl.semaphore_signal(barrier, inc=1, device_id=(row + 1, group), device_id_type=MESH)

    def pack(index, carry):
        packed[0, index] = a_ref[plan_ref[0, index]]
        packed[1, index] = a_ref[plan_ref[1, index]]
        return carry

    lax.fori_loop(0, size, pack, 0, unroll=2)

    pl.semaphore_wait(barrier, has_left.astype(jnp.int32) + has_right.astype(jnp.int32))

    def copy(side, other):
        return pltpu.make_async_remote_copy(
            src_ref=packed.at[side],
            dst_ref=out_ref.at[1 - side, pl.ds(0, size)],
            send_sem=send_sems.at[side],
            recv_sem=recv_sems.at[1 - side],
            device_id=(other, group),
            device_id_type=MESH,
        )

    @pl.when(has_left)
    def _():
        copy(0, row - 1).start()

    @pl.when(has_right)
    def _():
        copy(1, row + 1).start()

    @pl.when(has_left)
    def _():
        copy(0, row - 1).wait_send()
        copy(1, row - 1).wait_recv()

    @pl.when(has_right)
    def _():
        copy(1, row + 1).wait_send()
        copy(0, row + 1).wait_recv()


def product_kernel(dims, code_ref, cols_ref, r_ref, a_ref, halo_ref, out_ref, tiles_ref, jobs, sems):
    rows, groups, local_rows, op_slots, r_slots, cap, half = dims
    width = 2 * half
    tiles = local_rows * op_slots
    row_count = cols_ref.shape[0]
    own_cap = cap // groups
    row = lax.axis_index("rows")
    group = lax.axis_index("inner")
    own = pltpu.make_async_copy(a_ref, tiles_ref.at[pl.ds(0, tiles)], sems.at[0])
    near = pltpu.make_async_copy(halo_ref, tiles_ref.at[pl.ds(tiles, 2 * tiles)], sems.at[1])
    own.start()
    near.start()
    last = groups * row_count * own_cap
    scale = 1 << (3 * tiles * cap - 1).bit_length()

    def clear(index, carry):
        out_ref[index] = jnp.zeros(out_ref.shape[1:], jnp.float32)
        return carry

    lax.fori_loop(0, last, clear, 0, unroll=4)

    def list_row(c, found):
        def list_slot(j, found):
            fine = cols_ref[c, j]
            side = fine // (local_rows * groups) - row
            base = jnp.where(side == 0, width, jnp.where(side < 0, 0, half))
            base = base + lax.rem(fine, local_rows) * op_slots
            for t in range(op_slots):
                code = code_ref[c, base + t]
                jobs[found] = (c * r_slots + j) * scale + code
                found = found + (code >= 0).astype(jnp.int32)
            return found

        return lax.fori_loop(0, r_slots, list_slot, found)

    found = lax.fori_loop(0, row_count, list_row, jnp.int32(0))
    for extra in range(BATCH):
        jobs[found + extra] = -1
    own.wait()
    near.wait()

    def batch(step, carry):
        results = []
        targets = []
        for extra in range(BATCH):
            job = jobs[step * BATCH + extra]
            valid = job >= 0
            job = jnp.maximum(job, 0)
            pair = job // scale
            code = lax.rem(job, scale)
            slot = lax.rem(code, cap)
            ahead = lax.rem(slot // own_cap + groups - group, groups)
            target = (ahead * row_count + pair // r_slots) * own_cap + lax.rem(slot, own_cap)
            targets.append(jnp.where(valid, target, last))
            results.append(
                jnp.dot(
                    r_ref[pair],
                    tiles_ref[code // cap],
                    preferred_element_type=jnp.float32,
                )
            )
        for extra in range(BATCH):
            target = targets[extra]
            out_ref[target] = out_ref[target] + results[extra]
        return carry

    lax.fori_loop(0, (found + BATCH - 1) // BATCH, batch, 0)


def sum_kernel(groups, own, part_ref, landed, send_sems, recv_sems):
    row = lax.axis_index("rows")
    group = lax.axis_index("inner")
    barrier = pltpu.get_barrier_semaphore()
    for ahead in range(1, groups):
        pl.semaphore_signal(
            barrier, inc=1, device_id=(row, lax.rem(group + ahead, groups)), device_id_type=MESH
        )
    pl.semaphore_wait(barrier, groups - 1)
    copies = []
    for ahead in range(1, groups):
        copy = pltpu.make_async_remote_copy(
            src_ref=part_ref.at[pl.ds(ahead * own, own)],
            dst_ref=landed.at[ahead - 1],
            send_sem=send_sems.at[ahead - 1],
            recv_sem=recv_sems.at[ahead - 1],
            device_id=(row, lax.rem(group + ahead, groups)),
            device_id_type=MESH,
        )
        copy.start()
        copies.append(copy)
    for copy in copies:
        copy.wait()


def sizes_for(tiles):
    steps = [16, 18, 20, 21, 22, 23, 24, 25, 26, 27, 28, 29, 30, 32, 36, 42]
    return [size for size in steps if size < tiles] + [tiles]


def plain_body(rows, groups, r_tiles, r_cols, a_tiles, a_cols, c_cols, c_counts):
    local_rows, op_slots, tile, _ = a_tiles.shape
    row_count, r_slots = r_tiles.shape[:2]
    cap = c_cols.shape[1]
    tiles = local_rows * op_slots
    half = -(-tiles // 64) * 64
    width = 2 * half
    count = rows * groups
    own_cap = cap // groups
    dims = (rows, groups, local_rows, op_slots, r_slots, cap, half)
    vmem = pl.BlockSpec(memory_space=pltpu.VMEM)
    smem = pl.BlockSpec(memory_space=pltpu.SMEM)
    anywhere = pl.BlockSpec(memory_space=pl.ANY)

    flat = a_cols.reshape(count, tiles)
    flat = jnp.pad(flat, ((0, 0), (0, half - tiles)), constant_values=-2)
    columns = jnp.concatenate([flat, flat], axis=1)

    code, plan = pl.pallas_call(
        functools.partial(plan_kernel, dims),
        out_shape=(
            jax.ShapeDtypeStruct((row_count, 2 * width), jnp.int32),
            jax.ShapeDtypeStruct((8, width), jnp.int32),
        ),
        in_specs=[vmem] * 4,
        out_specs=(vmem, vmem),
        scratch_shapes=[
            pltpu.VMEM((row_count, width), jnp.int32),
            pltpu.VMEM((count, row_count, width), jnp.int32),
            pltpu.VMEM((count, width), jnp.int32),
            pltpu.SemaphoreType.DMA,
            pltpu.SemaphoreType.DMA,
        ],
        compiler_params=pltpu.CompilerParams(collective_id=0, has_side_effects=True),
        name="plan",
    )(r_cols, c_cols, c_counts[None, :], columns)

    flat_a = a_tiles.reshape(tiles, tile, tile)
    sizes = sizes_for(tiles)

    def exchange(number, size, plan, flat_a):
        return pl.pallas_call(
            functools.partial(halo_kernel, rows, size),
            out_shape=jax.ShapeDtypeStruct((2, tiles, tile, tile), a_tiles.dtype),
            in_specs=[smem, vmem],
            out_specs=anywhere,
            scratch_shapes=[
                pltpu.VMEM((2, size, tile, tile), a_tiles.dtype),
                pltpu.SemaphoreType.DMA((2,)),
                pltpu.SemaphoreType.DMA((2,)),
            ],
            compiler_params=pltpu.CompilerParams(collective_id=number + 2, has_side_effects=True),
            name=f"halo{size}",
        )(plan, flat_a)

    halo = lax.switch(
        plan[3, 0],
        [functools.partial(exchange, number, size) for number, size in enumerate(sizes)],
        plan,
        flat_a,
    )

    slots = row_count * r_slots * op_slots + BATCH
    partial_value = pl.pallas_call(
        functools.partial(product_kernel, dims),
        out_shape=jax.ShapeDtypeStruct((row_count * cap + 1, tile, tile), jnp.float32),
        in_specs=[smem, smem, vmem, anywhere, anywhere],
        out_specs=vmem,
        scratch_shapes=[
            pltpu.VMEM((3 * tiles, tile, tile), a_tiles.dtype),
            pltpu.SMEM((slots,), jnp.int32),
            pltpu.SemaphoreType.DMA((2,)),
        ],
        name="products",
    )(
        code,
        r_cols,
        r_tiles.reshape(row_count * r_slots, tile, tile),
        flat_a,
        halo.reshape(2 * tiles, tile, tile),
    )

    own_count = row_count * own_cap
    landed = pl.pallas_call(
        functools.partial(sum_kernel, groups, own_count),
        out_shape=jax.ShapeDtypeStruct((groups - 1, own_count, tile, tile), jnp.float32),
        in_specs=[anywhere],
        out_specs=anywhere,
        scratch_shapes=[
            pltpu.SemaphoreType.DMA((groups - 1,)),
            pltpu.SemaphoreType.DMA((groups - 1,)),
        ],
        compiler_params=pltpu.CompilerParams(collective_id=1, has_side_effects=True),
        name="sums",
    )(partial_value)
    c_tiles = partial_value[:own_count]
    for ahead in range(groups - 1):
        c_tiles = c_tiles + landed[ahead]
    c_tiles = c_tiles.astype(jnp.bfloat16)
    return (c_tiles.reshape(row_count, own_cap, tile, tile), plan[2, :row_count])

NEAR_SLOTS = 30
FAR_SLOTS = 21
CHUNK = 3
REMOTE = 1 << 14


def fused_kernel(
    dims, r_cols_ref, c_cols_ref, counts_ref, columns_ref, a_ref, r_ref,
    out_ref, offsets_ref, flag_ref,
    meta, gathered, close, pair_a, pair_r, packed, landed, sums, done, tables, codes, picks,
    local_sems, gather_sems, close_sems, pair_sems, near_sems, near_pair_sems, far_sems,
    far_pair_sems, table_sems, out_sems,
):
    (rows, groups, local_rows, op_slots, r_slots, cap, width, near_slots, far_slots, chunk) = dims
    count = rows * groups
    pairs = groups // 2
    tiles = local_rows * op_slots
    span = 2 * local_rows
    own_cap = cap // groups
    half_cap = cap // 2
    row_count = r_cols_ref.shape[0]
    live = r_slots + cap
    near_chunks = near_slots // chunk
    far_chunks = far_slots // chunk
    far_base = 2 * near_slots
    zero_near = 2 * (near_slots + far_slots)
    zero_own = 2 * tiles

    row = lax.axis_index("rows")
    group = lax.axis_index("inner")
    me = row * groups + group
    part = lax.rem(group, 2)
    first_group = group - part
    mate = first_group + 1 - part
    odd = lax.rem(row, 2)
    near = row + 1 - 2 * odd
    far = row - 1 + 2 * odd
    has_far = (far >= 0) & (far < rows)
    onward = near + 1 - 2 * odd
    has_onward = (onward >= 0) & (onward < rows)

    def remote(src, dst, send_sem, recv_sem, place):
        return pltpu.make_async_remote_copy(
            src_ref=src, dst_ref=dst, send_sem=send_sem, recv_sem=recv_sem,
            device_id=place, device_id_type=MESH,
        )

    own_a = pltpu.make_async_copy(
        a_ref, pair_a.at[pl.ds(part * tiles, tiles)], local_sems.at[0]
    )
    own_r = pltpu.make_async_copy(r_ref, pair_r.at[part], local_sems.at[1])
    own_a.start()
    own_r.start()

    barrier = pltpu.get_barrier_semaphore()

    def place(step):
        other = lax.rem(me + step, count)
        return (other // groups, lax.rem(other, groups))

    def greet(step, carry):
        pl.semaphore_signal(barrier, inc=1, device_id=place(step), device_id_type=MESH)
        return carry

    lax.fori_loop(1, count, greet, 0)

    small = (row_count, row_count)
    diagonal = lax.broadcasted_iota(jnp.int32, small, 0) == lax.broadcasted_iota(jnp.int32, small, 1)
    spread_counts = jnp.broadcast_to(counts_ref[...], small)
    own_counts = jnp.sum(jnp.where(diagonal, spread_counts, 0), axis=1, keepdims=True)
    meta[...] = jnp.full(meta.shape, -9, jnp.int32)
    meta[:, 0:r_slots] = r_cols_ref[...]
    meta[:, r_slots:live] = c_cols_ref[...]
    meta[:, live : live + 1] = own_counts
    gathered[me] = meta[...]
    pair_a[zero_own] = jnp.zeros(pair_a.shape[1:], pair_a.dtype)
    landed[zero_near] = jnp.zeros(landed.shape[1:], landed.dtype)

    pl.semaphore_wait(barrier, count - 1)

    mate_place = (row, mate)

    def to_close(slot, place):
        return remote(meta, close.at[slot], close_sems.at[0, slot], close_sems.at[1, slot], place)

    def start_close(target, first):
        for core in range(2):
            pltpu.make_async_remote_copy(
                src_ref=meta, dst_ref=close.at[first + part],
                send_sem=close_sems.at[0, first + core], recv_sem=close_sems.at[1, first + part],
                device_id=(target, first_group + core), device_id_type=MESH,
            ).start()

    def wait_close_recv(first):
        for core in range(2):
            to_close(first + core, mate_place).wait_recv()

    def wait_close_send(first):
        for core in range(2):
            to_close(first + core, mate_place).wait_send()

    start_close(near, 0)

    @pl.when(has_far)
    def _():
        start_close(far, 2)

    mate_a = remote(
        a_ref, pair_a.at[pl.ds(part * tiles, tiles)], pair_sems.at[0, 0], pair_sems.at[1, 0], mate_place
    )
    mate_a.start()

    def post(step, carry):
        remote(meta, gathered.at[me], gather_sems.at[0], gather_sems.at[1], place(step)).start()
        return carry

    lax.fori_loop(1, count, post, 0)
    mate_r = remote(r_ref, pair_r.at[part], pair_sems.at[0, 1], pair_sems.at[1, 1], mate_place)
    mate_r.start()

    lanes = lax.broadcasted_iota(jnp.int32, (1, width), 1)
    deep = lax.broadcasted_iota(jnp.int32, (op_slots, width), 0)
    wide = lax.broadcasted_iota(jnp.int32, (op_slots, width), 1)
    real = lanes < op_slots * span
    lane_fine = jnp.where(real, lax.rem(lanes, span), -(1 << 24))
    lane_core = lax.rem(lanes, span) // local_rows
    lane_tile = lane_core * tiles + lax.rem(lanes, local_rows) * op_slots + lanes // span

    def pair_columns(which_row):
        return pair_columns_at((which_row * groups + first_group) * local_rows)

    def pair_columns_at(start):
        block = start // 128
        values = columns_ref[:, pl.ds(pl.multiple_of(block * 128, 128), 128)]
        if width > 128:
            values = jnp.concatenate([values] * (width // 128), axis=1)
        offset = start - block * 128
        total = jnp.zeros((1, width), jnp.int32)
        for t in range(op_slots):
            moved = pltpu.roll(values[t : t + 1, :], lax.rem(t * span - offset + 128 * width, width), 1)
            total = jnp.where(lanes // span == t, moved, total)
        return jnp.where(real, total, -2)

    def pair_fine(which_row):
        return lane_fine + (which_row * groups + first_group) * local_rows

    def need_of(meta_low, meta_high, columns, fine):
        named = fine == meta_low[:, 0:1]
        for j in range(1, r_slots):
            named = named | (fine == meta_low[:, j : j + 1])
        for j in range(r_slots):
            named = named | (fine == meta_high[:, j : j + 1])
        wanted = columns == meta_low[:, r_slots : r_slots + 1]
        for s in range(1, cap):
            wanted = wanted | (columns == meta_low[:, r_slots + s : r_slots + s + 1])
        return jnp.max((named & wanted).astype(jnp.int32), axis=0, keepdims=True)

    def before(need):
        total = need
        step = 1
        while step < width:
            total = total + jnp.where(lanes >= step, pltpu.roll(total, step, 1), 0)
            step *= 2
        return total - need

    def list_places(need_far, need_near):
        only = need_near * (1 - need_far)
        first = before(need_far)
        second = before(only) + jnp.sum(need_far, axis=1, keepdims=True)
        return jnp.where(need_far > 0, first, jnp.where(only > 0, second, -1))

    own_columns = pair_columns(row)
    own_fine = pair_fine(row)
    wait_close_recv(0)

    @pl.when(has_far)
    def _():
        wait_close_recv(2)

    @pl.when(jnp.logical_not(has_far))
    def _():
        close[2] = jnp.full(close.shape[1:], -9, jnp.int32)
        close[3] = jnp.full(close.shape[1:], -9, jnp.int32)

    need_near = need_of(close[0], close[1], own_columns, own_fine)
    need_far = need_of(close[2], close[3], own_columns, own_fine)
    places = list_places(need_far, need_near)
    pick_rows = -(-near_slots // 8) * 8
    slot_down = lax.broadcasted_iota(jnp.int32, (pick_rows, width), 0)
    chosen = jnp.broadcast_to(places, (pick_rows, width)) == 2 * slot_down + part
    picked = jnp.sum(
        jnp.where(chosen, jnp.broadcast_to(lane_tile, (pick_rows, width)), 0), axis=1, keepdims=True
    )
    across = lax.broadcasted_iota(jnp.int32, (pick_rows, width), 1)
    pick_row = jnp.sum(
        jnp.where(slot_down == across, jnp.broadcast_to(picked, (pick_rows, width)), 0),
        axis=0, keepdims=True,
    )
    tables[0:8, :] = jnp.broadcast_to(pick_row, (8, width))
    pick_copy = pltpu.make_async_copy(tables.at[pl.ds(0, 8)], picks, table_sems.at[0])
    pick_copy.start()
    own_a.wait()
    mate_a.wait_recv()
    pick_copy.wait()

    def near_copy(index):
        return remote(
            packed.at[pl.ds(index * chunk, chunk)],
            landed.at[pl.ds(part * near_slots + index * chunk, chunk)],
            near_sems.at[0, index], near_sems.at[1, index], (near, group),
        )

    def pack(index):
        for extra in range(chunk):
            packed[index * chunk + extra] = pair_a[picks[0, index * chunk + extra]]

    pack(0)
    for index in range(near_chunks):
        if index + 1 < near_chunks:
            pack(index + 1)
        near_copy(index).start()

    everyone = gathered.at[pl.ds(0, count - 1)]
    gather_all = pltpu.make_async_copy(everyone, everyone, gather_sems.at[1])
    gather_all.wait()

    def gathered_pair(which_row):
        safe = jnp.clip(which_row, 0, rows - 1)
        base = safe * groups + first_group
        return gathered[base], gathered[base + 1]

    my_low, my_high = gathered_pair(row)
    near_columns = pair_columns(near)
    near_fine = pair_fine(near)
    far_row = jnp.clip(far, 0, rows - 1)
    far_columns = pair_columns(far_row)
    far_fine = jnp.where(has_far, pair_fine(far_row), -(1 << 24))
    past_low, past_high = gathered_pair(onward)
    past = need_of(past_low, past_high, near_columns, near_fine)
    past = jnp.where(has_onward, past, 0)
    near_places = list_places(past, need_of(my_low, my_high, near_columns, near_fine))
    far_need = need_of(my_low, my_high, far_columns, far_fine)
    far_places = jnp.where(far_need > 0, before(far_need), -1)

    def landing(places, slots, base):
        fits = (places >= 0) & (places < 2 * slots)
        at = base + lax.rem(places, 2) * slots + places // 2
        return jnp.where(fits, REMOTE + at, -1)

    near_at = landing(near_places, near_slots, 0)
    far_at = landing(far_places, far_slots, far_base)

    above = (row_count, width)
    table_lanes = lax.broadcasted_iota(jnp.int32, above, 1)
    own_at, near_at, far_at = [jnp.broadcast_to(x, above) for x in (lane_tile, near_at, far_at)]
    slot_own, slot_near, slot_far = [], [], []
    for index in range(half_cap):
        even = (2 * (index // own_cap)) * own_cap + index % own_cap
        low = my_low[:, r_slots + even : r_slots + even + 1]
        high = my_low[:, r_slots + even + own_cap : r_slots + even + own_cap + 1]
        column = jnp.where(part == 0, low, high)
        slot_own.append(jnp.where(own_columns == column, own_at, -1))
        slot_near.append(jnp.where(near_columns == column, near_at, -1))
        slot_far.append(jnp.where(far_columns == column, far_at, -1))
    code = jnp.full(above, -1, jnp.int32)
    for j in range(2 * r_slots):
        block = my_low if j < r_slots else my_high
        named = block[:, j % r_slots : j % r_slots + 1]
        in_own = own_fine == named
        in_near = near_fine == named
        in_far = far_fine == named
        for index in range(half_cap):
            found = jnp.where(in_own, slot_own[index], -1)
            found = jnp.where(in_near, slot_near[index], found)
            found = jnp.where(in_far, slot_far[index], found)
            best = jnp.max(found, axis=1, keepdims=True)
            code = jnp.where(table_lanes == index * 2 * r_slots + j, best, code)
    tables[0:row_count, :] = jnp.where((code >= 0) & (code < REMOTE), code, zero_own)
    tables[row_count : 2 * row_count, :] = jnp.where(code >= REMOTE, code - REMOTE, zero_near)
    code_copy = pltpu.make_async_copy(tables, codes, table_sems.at[1])
    code_copy.start()

    def earlier(index, total):
        block = gathered[index * groups]
        return total + jnp.sum(block[:, live : live + 1], axis=0, keepdims=True)

    first = lax.fori_loop(0, row, earlier, jnp.zeros((1, 1), jnp.int32))
    counts = jnp.broadcast_to(own_counts, small)
    inner_sum = jnp.sum(
        jnp.where(
            lax.broadcasted_iota(jnp.int32, small, 0) < lax.broadcasted_iota(jnp.int32, small, 1),
            counts, 0,
        ),
        axis=0, keepdims=True,
    )
    offsets_ref[...] = inner_sum + first
    code_copy.wait()
    own_r.wait()
    mate_r.wait_recv()

    tile = pair_a.shape[1:]

    def multiply(c, stage, index, source):
        total = None
        for j in range(0, 2 * r_slots, 2):
            left = jnp.concatenate(
                [pair_r[x // r_slots, c * r_slots + x % r_slots] for x in (j, j + 1)], axis=1
            )
            right = jnp.concatenate(
                [
                    jnp.concatenate(
                        [
                            source[codes[stage * row_count + c, slot * 2 * r_slots + x]]
                            for slot in (index, index + 1)
                        ],
                        axis=1,
                    )
                    for x in (j, j + 1)
                ],
                axis=0,
            )
            term = jnp.dot(left, right, preferred_element_type=jnp.float32)
            total = term if total is None else total + term
        return total

    def own_stage(c, carry):
        for index in range(0, half_cap, 2):
            sums[c * half_cap // 2 + index // 2] = multiply(c, 0, index, pair_a)
        return carry

    lax.fori_loop(0, row_count, own_stage, 0)

    def near_mate(index):
        view = landed.at[pl.ds(part * near_slots + index * chunk, chunk)]
        return remote(view, view, near_pair_sems.at[0, index], near_pair_sems.at[1, index], mate_place)

    def far_view(index):
        return landed.at[pl.ds(far_base + part * far_slots + index * chunk, chunk)]

    def far_copy(index):
        return remote(
            landed.at[pl.ds(part * near_slots + index * chunk, chunk)], far_view(index),
            far_sems.at[0, index], far_sems.at[1, index], (onward, group),
        )

    def far_mate(index):
        view = far_view(index)
        return remote(
            view, view, far_pair_sems.at[0, index], far_pair_sems.at[1, index], mate_place
        )

    def take_far(index):
        @pl.when(has_far)
        def _():
            far_copy(index).wait_recv()
            far_mate(index).start()

    lag = 2
    for index in range(near_chunks):
        near_copy(index).wait_recv()
        if index < far_chunks:
            @pl.when(has_onward)
            def _():
                far_copy(index).start()
        near_mate(index).start()
        if 0 <= index - lag < far_chunks:
            take_far(index - lag)
    for index in range(max(near_chunks - lag, 0), far_chunks):
        take_far(index)

    pair_count = rows * pairs

    def crowd(which, most):
        which_row = which // pairs
        base_group = 2 * lax.rem(which, pairs)
        parity = lax.rem(which_row, 2)
        which_near = which_row + 1 - 2 * parity
        which_far = which_row - 1 + 2 * parity
        far_there = (which_far >= 0) & (which_far < rows)
        start = (which_row * groups + base_group) * local_rows
        columns = pair_columns_at(start)
        fine = lane_fine + start
        near_base = which_near * groups + base_group
        far_base_at = jnp.clip(which_far, 0, rows - 1) * groups + base_group
        by_near = need_of(gathered[near_base], gathered[near_base + 1], columns, fine)
        by_far = need_of(gathered[far_base_at], gathered[far_base_at + 1], columns, fine)
        by_far = jnp.where(far_there, by_far, 0)
        sends = jnp.sum(jnp.maximum(by_near, by_far), axis=1, keepdims=True)
        passes = jnp.sum(by_far, axis=1, keepdims=True)
        over = jnp.maximum(sends - 2 * near_slots, passes - 2 * far_slots)
        return jnp.maximum(most, over)

    worst_over = lax.fori_loop(0, pair_count, crowd, jnp.full((1, 1), -1, jnp.int32))
    flag_ref[...] = (worst_over > 0).astype(jnp.int32)

    for index in range(near_chunks):
        near_mate(index).wait_recv()

    @pl.when(has_far)
    def _():
        for index in range(far_chunks):
            far_mate(index).wait_recv()

    ahead_of = [lax.rem(index // own_cap + pairs - group // 2, pairs) for index in range(half_cap)]

    def out_copy(c, index):
        return pltpu.make_async_copy(
            done.at[c * half_cap + index],
            out_ref.at[ahead_of[index] * row_count * own_cap + c * own_cap + index % own_cap],
            out_sems.at[c * half_cap + index],
        )

    def near_stage(c, carry):
        for index in range(0, half_cap, 2):
            total = sums[c * half_cap // 2 + index // 2] + multiply(c, 1, index, landed)
            total = total.astype(done.dtype)
            done[c * half_cap + index] = total[:, : tile[1]]
            done[c * half_cap + index + 1] = total[:, tile[1] :]
        for index in range(half_cap):
            out_copy(c, index).start()
        return carry

    lax.fori_loop(0, row_count, near_stage, 0)

    sent = gathered.at[pl.ds(0, count - 1)]
    pltpu.make_async_copy(sent, sent, gather_sems.at[0]).wait()
    wait_close_send(0)

    @pl.when(has_far)
    def _():
        wait_close_send(2)

    mate_a.wait_send()
    mate_r.wait_send()
    for index in range(near_chunks):
        near_copy(index).wait_send()
        near_mate(index).wait_send()

    @pl.when(has_onward)
    def _():
        for index in range(far_chunks):
            far_copy(index).wait_send()

    @pl.when(has_far)
    def _():
        for index in range(far_chunks):
            far_mate(index).wait_send()

    def finish(c, carry):
        for index in range(half_cap):
            out_copy(c, index).wait()
        return carry

    lax.fori_loop(0, row_count, finish, 0)


def pair_sum_kernel(pairs, own, part_ref, landed, send_sems, recv_sems):
    row = lax.axis_index("rows")
    group = lax.axis_index("inner")
    core = lax.rem(group, 2)
    barrier = pltpu.get_barrier_semaphore()

    def place(ahead):
        return (row, 2 * lax.rem(group // 2 + ahead, pairs) + core)

    for ahead in range(1, pairs):
        pl.semaphore_signal(barrier, inc=1, device_id=place(ahead), device_id_type=MESH)
    pl.semaphore_wait(barrier, pairs - 1)
    copies = []
    for ahead in range(1, pairs):
        copy = pltpu.make_async_remote_copy(
            src_ref=part_ref.at[pl.ds(ahead * own, own)],
            dst_ref=landed.at[ahead - 1],
            send_sem=send_sems.at[ahead - 1],
            recv_sem=recv_sems.at[ahead - 1],
            device_id=place(ahead),
            device_id_type=MESH,
        )
        copy.start()
        copies.append(copy)
    for copy in copies:
        copy.wait()


def fused_body(rows, groups, r_tiles, r_cols, a_tiles, a_cols, c_cols, c_counts):
    local_rows, op_slots, tile, _ = a_tiles.shape
    row_count, r_slots = r_tiles.shape[:2]
    cap = c_cols.shape[1]
    tiles = local_rows * op_slots
    pairs = groups // 2
    count = rows * groups
    own_cap = cap // groups
    half_cap = cap // 2
    width = -(-2 * tiles // 128) * 128
    near_slots = min(NEAR_SLOTS, -(-tiles // CHUNK) * CHUNK)
    far_slots = min(FAR_SLOTS, near_slots)
    dims = (rows, groups, local_rows, op_slots, r_slots, cap, width, near_slots, far_slots, CHUNK)
    near_chunks = near_slots // CHUNK
    far_chunks = far_slots // CHUNK
    dtype = a_tiles.dtype
    out_dtype = jnp.bfloat16 if pairs == 1 else jnp.float32
    own = row_count * own_cap
    vmem = pl.BlockSpec(memory_space=pltpu.VMEM)
    anywhere = pl.BlockSpec(memory_space=pl.ANY)
    dma = pltpu.SemaphoreType.DMA
    part, offsets, flag = pl.pallas_call(
        functools.partial(fused_kernel, dims),
        out_shape=(
            jax.ShapeDtypeStruct((pairs * own, tile, tile), out_dtype),
            jax.ShapeDtypeStruct((1, row_count), jnp.int32),
            jax.ShapeDtypeStruct((1, 1), jnp.int32),
        ),
        in_specs=[vmem] * 4 + [anywhere] * 2,
        out_specs=(anywhere, vmem, vmem),
        scratch_shapes=[
            pltpu.VMEM((row_count, 128), jnp.int32),
            pltpu.VMEM((count, row_count, 128), jnp.int32),
            pltpu.VMEM((4, row_count, 128), jnp.int32),
            pltpu.VMEM((2 * tiles + 1, tile, tile), dtype),
            pltpu.VMEM((2, row_count * r_slots, tile, tile), dtype),
            pltpu.VMEM((near_slots, tile, tile), dtype),
            pltpu.VMEM((2 * (near_slots + far_slots) + 1, tile, tile), dtype),
            pltpu.VMEM((row_count * half_cap // 2, tile, 2 * tile), jnp.float32),
            pltpu.VMEM((row_count * half_cap, tile, tile), out_dtype),
            pltpu.VMEM((2 * row_count, width), jnp.int32),
            pltpu.SMEM((2 * row_count, width), jnp.int32),
            pltpu.SMEM((8, width), jnp.int32),
            dma((2,)),
            dma((2,)),
            dma((2, 4)),
            dma((2, 2)),
            dma((2, near_chunks)),
            dma((2, near_chunks)),
            dma((2, far_chunks)),
            dma((2, far_chunks)),
            dma((2,)),
            dma((row_count * half_cap,)),
        ],
        compiler_params=pltpu.CompilerParams(collective_id=40, has_side_effects=True),
        name="fused",
    )(
        r_cols,
        c_cols,
        c_counts[None, :],
        a_cols.T,
        a_tiles.reshape(tiles, tile, tile),
        r_tiles.reshape(row_count * r_slots, tile, tile),
    )
    if pairs == 1:
        c_tiles = part
    else:
        landed = pl.pallas_call(
            functools.partial(pair_sum_kernel, pairs, own),
            out_shape=jax.ShapeDtypeStruct((pairs - 1, own, tile, tile), jnp.float32),
            in_specs=[anywhere],
            out_specs=anywhere,
            scratch_shapes=[dma((pairs - 1,)), dma((pairs - 1,))],
            compiler_params=pltpu.CompilerParams(collective_id=41, has_side_effects=True),
            name="pair_sums",
        )(part)
        c_tiles = part[:own]
        for ahead in range(pairs - 1):
            c_tiles = c_tiles + landed[ahead]
        c_tiles = c_tiles.astype(jnp.bfloat16)
    return c_tiles.reshape(row_count, own_cap, tile, tile), offsets[0], flag[0, 0]


def body(rows, groups, *args):
    if rows % 2 or groups % 2:
        return plain_body(rows, groups, *args)
    c_tiles, offsets, flag = fused_body(rows, groups, *args)

    def again(c_tiles, offsets, *args):
        return plain_body(rows, groups, *args)

    def keep(c_tiles, offsets, *args):
        return c_tiles, offsets

    return lax.cond(flag > 0, again, keep, c_tiles, offsets, *args)


def solution(mesh):
    rows = mesh.shape["rows"]
    groups = mesh.shape["inner"]
    return jax.shard_map(
        functools.partial(body, rows, groups),
        mesh=mesh,
        in_specs=(
            P("rows", "inner", None, None),
            P("rows", "inner"),
            P(("rows", "inner"), None, None, None),
            P(),
            P("rows", None),
            P("rows"),
        ),
        out_specs=(P("rows", "inner", None, None), P("rows")),
        check_vma=False,
    )
```

profile of v0, /device:TPU:0, one launch (start us, length us, event | category | flops | bytes accessed | tf_op | source)
XLA Modules:
  0.0 49.0 jit_solution(10820601434437513723)
XLA Ops:
  0.6 0.0 copy-start.4
  0.6 0.0 copy-start.3
  0.7 0.0 copy-start.2
  0.7 0.0 copy-start
  0.7 0.0 copy-start.1
  0.7 46.1 %fused.1 = (bf16[32,128,128]{2,1,0:T(8,128)(2,1)S(1)}, s32[1,8]{1,0:T(1,128)S(1)}, s32[1,1]{1,0:T(1,128)}) custom-call(s32[8,8]{1,0:T(8,128)} %r_cols_ref.1, s32[8,8]{1,0:T(8,128)} %c_cols_ref.1, s32[1,8]{1,0:T(1,128)} %bitcast.74, s32[7,256]{1,0:T(8,128)} %bitcast.73, bf16[56,128,128]{2,1,0:T(8,128)(2,1)} %bitcast.33, bf16[64,128,128]{2,1,0:T(8,128)(2,1)} %bitcast.69), custom_call_target="tpu_custom_call" | custom-call | tf_op jit(solution)/shard_map/fused/pallas_call | solution.py:910
  47.4 0.0 copy-done.4
  47.4 0.0 copy-done.3
  47.4 0.0 copy-done.2
  47.5 0.0 copy-done
  47.5 0.0 copy-done.1
  47.5 1.0 %copy.33 = bf16[8,4,128,128]{3,2,1,0:T(8,128)(2,1)} copy(bf16[8,4,128,128]{3,2,1,0:T(8,128)(2,1)S(1)} %get-tuple-element.183) | data formatting | bytes 2097152
  48.5 0.5 %copy.34 = s32[8]{0:T(128)} copy(s32[8]{0:T(128)S(1)} %get-tuple-element.184) | data formatting | bytes 64
  (1 shorter events, 0.0 us)
Async XLA Ops:
  0.6 46.8 %copy-start.4 = (s32[8]{0:T(128)S(1)}, s32[8]{0:T(128)}, u32[]{:S(2)}) copy-start(s32[8]{0:T(128)} %param.30) | copy-start | bytes 100
  0.6 46.8 %copy-start.3 = (s32[8,8]{1,0:T(8,128)S(1)}, s32[8,8]{1,0:T(8,128)}, u32[]{:S(2)}) copy-start(s32[8,8]{1,0:T(8,128)} %c_cols_ref.1) | copy-start | bytes 772
  0.7 46.8 %copy-start.2 = (s32[256,7]{0,1:T(8,128)S(1)}, s32[256,7]{0,1:T(8,128)}, u32[]{:S(2)}) copy-start(s32[256,7]{0,1:T(8,128)} %param.28) | copy-start | bytes 21508
  0.7 46.8 %copy-start = (bf16[8,7,128,128]{3,2,1,0:T(8,128)(2,1)S(1)}, bf16[8,7,128,128]{3,2,1,0:T(8,128)(2,1)}, u32[]{:S(2)}) copy-start(bf16[8,7,128,128]{3,2,1,0:T(8,128)(2,1)} %param.27) | copy-start | bytes 5505028
  0.7 46.8 %copy-start.1 = (s32[8,8]{1,0:T(8,128)S(1)}, s32[8,8]{1,0:T(8,128)}, u32[]{:S(2)}) copy-start(s32[8,8]{1,0:T(8,128)} %r_cols_ref.1) | copy-start | bytes 772
where the time goes:
time: 49.2 us; the launch traced here: 49 us
  Pallas kernels  46.1 us (94%)
  local copies, waits for them, and re-layouts  1.5 us (3%)
  between operations  1.4 us (3%)
    pallas_call x1, Pallas kernels, fused_body(): pl.pallas_call(functools.partial(fused_kernel, dims), out_shape=(jax.Shap...  46.1 us
    unnamed x12, local copies, waits for them, and re-layouts  1.5 us

commit v1 on v0

--- a/solution.py
+++ b/solution.py
@@ -402,37 +402,43 @@
     c_tiles = c_tiles.astype(jnp.bfloat16)
     return (c_tiles.reshape(row_count, own_cap, tile, tile), plan[2, :row_count])
 
-NEAR_SLOTS = 30
-FAR_SLOTS = 21
+LIST_SLOTS = 27
+PASS_SLOTS = 15
 CHUNK = 3
+JOBS = 6
 REMOTE = 1 << 14
 
 
 def fused_kernel(
-    dims, r_cols_ref, c_cols_ref, counts_ref, columns_ref, a_ref, r_ref,
+    dims, r_cols_hbm, c_cols_hbm, counts_hbm, columns_hbm, a_ref, r_ref,
     out_ref, offsets_ref, flag_ref,
-    meta, gathered, close, pair_a, pair_r, packed, landed, sums, done, tables, codes, picks,
-    local_sems, gather_sems, close_sems, pair_sems, near_sems, near_pair_sems, far_sems,
-    far_pair_sems, table_sems, out_sems,
+    r_cols_ref, c_cols_ref, counts_ref, columns_ref,
+    meta, close, placing, pair_a, pair_r, packed, landed, sums, tables, codes, picks,
+    told, scan_out, scan_in,
+    local_sems, close_sems, pair_sems, place_sems, early_sems, near_sems, near_send,
+    near_pair_sems, far_sems, far_send, far_pair_sems, table_sems, told_sems, scan_sems,
 ):
-    (rows, groups, local_rows, op_slots, r_slots, cap, width, near_slots, far_slots, chunk) = dims
-    count = rows * groups
+    (rows, groups, local_rows, op_slots, r_slots, cap, width, list_slots, pass_slots, chunk) = dims
     pairs = groups // 2
     tiles = local_rows * op_slots
     span = 2 * local_rows
     own_cap = cap // groups
     half_cap = cap // 2
+    both = 2 * r_slots
     row_count = r_cols_ref.shape[0]
     live = r_slots + cap
-    near_chunks = near_slots // chunk
-    far_chunks = far_slots // chunk
+    early = op_slots
+    near_slots = early + list_slots
+    far_slots = early + pass_slots
+    near_chunks = list_slots // chunk
+    far_chunks = pass_slots // chunk
     far_base = 2 * near_slots
     zero_near = 2 * (near_slots + far_slots)
     zero_own = 2 * tiles
+    rounds = (rows - 1).bit_length()
 
     row = lax.axis_index("rows")
     group = lax.axis_index("inner")
-    me = row * groups + group
     part = lax.rem(group, 2)
     first_group = group - part
     mate = first_group + 1 - part
@@ -442,13 +448,37 @@
     has_far = (far >= 0) & (far < rows)
     onward = near + 1 - 2 * odd
     has_onward = (onward >= 0) & (onward < rows)
-
-    def remote(src, dst, send_sem, recv_sem, place):
-        return pltpu.make_async_remote_copy(
-            src_ref=src, dst_ref=dst, send_sem=send_sem, recv_sem=recv_sem,
-            device_id=place, device_id_type=MESH,
-        )
-
+    mate_place = (row, mate)
+
+    barrier = pltpu.get_barrier_semaphore()
+
+    def greet(place):
+        pl.semaphore_signal(barrier, inc=1, device_id=place, device_id_type=MESH)
+
+    for core in range(2):
+        greet((near, first_group + core))
+
+    @pl.when(has_far)
+    def _():
+        for core in range(2):
+            greet((far, first_group + core))
+
+    for ahead in range(1, groups):
+        greet((row, lax.rem(group + ahead, groups)))
+
+    small_copies = [
+        pltpu.make_async_copy(src, dst, local_sems.at[2 + index])
+        for index, (src, dst) in enumerate(
+            [
+                (r_cols_hbm, r_cols_ref),
+                (c_cols_hbm, c_cols_ref),
+                (counts_hbm, counts_ref),
+                (columns_hbm, columns_ref),
+            ]
+        )
+    ]
+    for copy in small_copies:
+        copy.start()
     own_a = pltpu.make_async_copy(
         a_ref, pair_a.at[pl.ds(part * tiles, tiles)], local_sems.at[0]
     )
@@ -456,84 +486,68 @@
     own_a.start()
     own_r.start()
 
-    barrier = pltpu.get_barrier_semaphore()
-
-    def place(step):
-        other = lax.rem(me + step, count)
-        return (other // groups, lax.rem(other, groups))
-
-    def greet(step, carry):
-        pl.semaphore_signal(barrier, inc=1, device_id=place(step), device_id_type=MESH)
-        return carry
-
-    lax.fori_loop(1, count, greet, 0)
+    def remote(src, dst, send_sem, recv_sem, place):
+        return pltpu.make_async_remote_copy(
+            src_ref=src, dst_ref=dst, send_sem=send_sem, recv_sem=recv_sem,
+            device_id=place, device_id_type=MESH,
+        )
+
+    def wait_bytes(view, sem):
+        pltpu.make_async_copy(view, view, sem).wait()
 
     small = (row_count, row_count)
     diagonal = lax.broadcasted_iota(jnp.int32, small, 0) == lax.broadcasted_iota(jnp.int32, small, 1)
+    meta[...] = jnp.full(meta.shape, -9, jnp.int32)
+    pair_a[zero_own] = jnp.zeros(pair_a.shape[1:], pair_a.dtype)
+    landed[zero_near] = jnp.zeros(landed.shape[1:], landed.dtype)
+    for copy in small_copies:
+        copy.wait()
     spread_counts = jnp.broadcast_to(counts_ref[...], small)
     own_counts = jnp.sum(jnp.where(diagonal, spread_counts, 0), axis=1, keepdims=True)
-    meta[...] = jnp.full(meta.shape, -9, jnp.int32)
     meta[:, 0:r_slots] = r_cols_ref[...]
     meta[:, r_slots:live] = c_cols_ref[...]
-    meta[:, live : live + 1] = own_counts
-    gathered[me] = meta[...]
-    pair_a[zero_own] = jnp.zeros(pair_a.shape[1:], pair_a.dtype)
-    landed[zero_near] = jnp.zeros(landed.shape[1:], landed.dtype)
-
-    pl.semaphore_wait(barrier, count - 1)
-
-    mate_place = (row, mate)
-
-    def to_close(slot, place):
-        return remote(meta, close.at[slot], close_sems.at[0, slot], close_sems.at[1, slot], place)
-
-    def start_close(target, first):
+    own_a.wait()
+
+    pl.semaphore_wait(barrier, groups + 1 + 2 * has_far.astype(jnp.int32))
+
+    def start_close(target, first, which):
         for core in range(2):
-            pltpu.make_async_remote_copy(
-                src_ref=meta, dst_ref=close.at[first + part],
-                send_sem=close_sems.at[0, first + core], recv_sem=close_sems.at[1, first + part],
-                device_id=(target, first_group + core), device_id_type=MESH,
+            remote(
+                meta, close.at[first + part], close_sems.at[0, which], close_sems.at[1, which],
+                (target, first_group + core),
             ).start()
 
-    def wait_close_recv(first):
-        for core in range(2):
-            to_close(first + core, mate_place).wait_recv()
-
-    def wait_close_send(first):
-        for core in range(2):
-            to_close(first + core, mate_place).wait_send()
-
-    start_close(near, 0)
-
     @pl.when(has_far)
     def _():
-        start_close(far, 2)
-
+        start_close(far, 2, 1)
+
+    start_close(near, 0, 0)
+    to_mate = remote(meta, close.at[4], close_sems.at[0, 2], close_sems.at[1, 2], mate_place)
+    to_mate.start()
     mate_a = remote(
         a_ref, pair_a.at[pl.ds(part * tiles, tiles)], pair_sems.at[0, 0], pair_sems.at[1, 0], mate_place
     )
     mate_a.start()
 
-    def post(step, carry):
-        remote(meta, gathered.at[me], gather_sems.at[0], gather_sems.at[1], place(step)).start()
-        return carry
-
-    lax.fori_loop(1, count, post, 0)
+    early_copy = remote(
+        pair_a.at[pl.ds(part * tiles, early)], landed.at[pl.ds(part * near_slots, early)],
+        early_sems.at[0], early_sems.at[1], (near, group),
+    )
+    early_copy.start()
     mate_r = remote(r_ref, pair_r.at[part], pair_sems.at[0, 1], pair_sems.at[1, 1], mate_place)
     mate_r.start()
 
     lanes = lax.broadcasted_iota(jnp.int32, (1, width), 1)
-    deep = lax.broadcasted_iota(jnp.int32, (op_slots, width), 0)
-    wide = lax.broadcasted_iota(jnp.int32, (op_slots, width), 1)
     real = lanes < op_slots * span
+    lane_slot = lanes // span
     lane_fine = jnp.where(real, lax.rem(lanes, span), -(1 << 24))
     lane_core = lax.rem(lanes, span) // local_rows
-    lane_tile = lane_core * tiles + lax.rem(lanes, local_rows) * op_slots + lanes // span
+    lane_local = lax.rem(lanes, local_rows)
+    lane_tile = lane_core * tiles + lane_local * op_slots + lane_slot
+    late = jnp.where(lane_local > 0, 1, 0)
 
     def pair_columns(which_row):
-        return pair_columns_at((which_row * groups + first_group) * local_rows)
-
-    def pair_columns_at(start):
+        start = (which_row * groups + first_group) * local_rows
         block = start // 128
         values = columns_ref[:, pl.ds(pl.multiple_of(block * 128, 128), 128)]
         if width > 128:
@@ -542,7 +556,7 @@
         total = jnp.zeros((1, width), jnp.int32)
         for t in range(op_slots):
             moved = pltpu.roll(values[t : t + 1, :], lax.rem(t * span - offset + 128 * width, width), 1)
-            total = jnp.where(lanes // span == t, moved, total)
+            total = jnp.where(lane_slot == t, moved, total)
         return jnp.where(real, total, -2)
 
     def pair_fine(which_row):
@@ -567,29 +581,35 @@
             step *= 2
         return total - need
 
-    def list_places(need_far, need_near):
-        only = need_near * (1 - need_far)
-        first = before(need_far)
-        second = before(only) + jnp.sum(need_far, axis=1, keepdims=True)
-        return jnp.where(need_far > 0, first, jnp.where(only > 0, second, -1))
+    def landing(places, count, base, slots):
+        fits = (places >= 0) & (places < 2 * count)
+        at = lax.rem(places, 2) * slots + early + places // 2
+        at = jnp.where(late > 0, jnp.where(fits, at, -1), lane_core * slots + lane_slot)
+        return jnp.where(real & (at >= 0), REMOTE + base + at, -1)
 
     own_columns = pair_columns(row)
     own_fine = pair_fine(row)
-    wait_close_recv(0)
 
     @pl.when(has_far)
     def _():
-        wait_close_recv(2)
+        wait_bytes(close.at[pl.ds(2, 2)], close_sems.at[1, 1])
 
     @pl.when(jnp.logical_not(has_far))
     def _():
         close[2] = jnp.full(close.shape[1:], -9, jnp.int32)
         close[3] = jnp.full(close.shape[1:], -9, jnp.int32)
 
-    need_near = need_of(close[0], close[1], own_columns, own_fine)
-    need_far = need_of(close[2], close[3], own_columns, own_fine)
-    places = list_places(need_far, need_near)
-    pick_rows = -(-near_slots // 8) * 8
+    need_far = need_of(close[2], close[3], own_columns, own_fine) * late
+    far_before = before(need_far)
+    far_total = jnp.sum(need_far, axis=1, keepdims=True)
+    wait_bytes(close.at[pl.ds(0, 2)], close_sems.at[1, 0])
+    need_near = need_of(close[0], close[1], own_columns, own_fine) * late
+    need_only = need_near * (1 - need_far)
+    near_total = far_total + jnp.sum(need_only, axis=1, keepdims=True)
+    places = jnp.where(
+        need_far > 0, far_before, jnp.where(need_only > 0, before(need_only) + far_total, -1)
+    )
+    pick_rows = -(-list_slots // 8) * 8
     slot_down = lax.broadcasted_iota(jnp.int32, (pick_rows, width), 0)
     chosen = jnp.broadcast_to(places, (pick_rows, width)) == 2 * slot_down + part
     picked = jnp.sum(
@@ -603,15 +623,19 @@
     tables[0:8, :] = jnp.broadcast_to(pick_row, (8, width))
     pick_copy = pltpu.make_async_copy(tables.at[pl.ds(0, 8)], picks, table_sems.at[0])
     pick_copy.start()
-    own_a.wait()
+    placing[0] = jnp.broadcast_to(landing(places, list_slots, 0, near_slots), placing.shape[1:])
+    place_copy = remote(placing.at[0], placing.at[1], place_sems.at[0], place_sems.at[1], (near, group))
+    place_copy.start()
     mate_a.wait_recv()
     pick_copy.wait()
 
+    def near_view(index):
+        return landed.at[pl.ds(part * near_slots + early + index * chunk, chunk)]
+
     def near_copy(index):
         return remote(
-            packed.at[pl.ds(index * chunk, chunk)],
-            landed.at[pl.ds(part * near_slots + index * chunk, chunk)],
-            near_sems.at[0, index], near_sems.at[1, index], (near, group),
+            packed.at[pl.ds(index * chunk, chunk)], near_view(index),
+            near_send.at[0], near_sems.at[index], (near, group),
         )
 
     def pack(index):
@@ -624,35 +648,20 @@
             pack(index + 1)
         near_copy(index).start()
 
-    everyone = gathered.at[pl.ds(0, count - 1)]
-    gather_all = pltpu.make_async_copy(everyone, everyone, gather_sems.at[1])
-    gather_all.wait()
-
-    def gathered_pair(which_row):
-        safe = jnp.clip(which_row, 0, rows - 1)
-        base = safe * groups + first_group
-        return gathered[base], gathered[base + 1]
-
-    my_low, my_high = gathered_pair(row)
     near_columns = pair_columns(near)
     near_fine = pair_fine(near)
     far_row = jnp.clip(far, 0, rows - 1)
     far_columns = pair_columns(far_row)
     far_fine = jnp.where(has_far, pair_fine(far_row), -(1 << 24))
-    past_low, past_high = gathered_pair(onward)
-    past = need_of(past_low, past_high, near_columns, near_fine)
-    past = jnp.where(has_onward, past, 0)
-    near_places = list_places(past, need_of(my_low, my_high, near_columns, near_fine))
-    far_need = need_of(my_low, my_high, far_columns, far_fine)
+    to_mate.wait_recv()
+    mine, other = meta[...], close[4]
+    my_low = jnp.where(part == 0, mine, other)
+    my_high = jnp.where(part == 0, other, mine)
+    far_need = need_of(my_low, my_high, far_columns, far_fine) * late
     far_places = jnp.where(far_need > 0, before(far_need), -1)
-
-    def landing(places, slots, base):
-        fits = (places >= 0) & (places < 2 * slots)
-        at = base + lax.rem(places, 2) * slots + places // 2
-        return jnp.where(fits, REMOTE + at, -1)
-
-    near_at = landing(near_places, near_slots, 0)
-    far_at = landing(far_places, far_slots, far_base)
+    far_at = landing(far_places, pass_slots, far_base, far_slots)
+    place_copy.wait_recv()
+    near_at = placing[1][0:1, :]
 
     above = (row_count, width)
     table_lanes = lax.broadcasted_iota(jnp.int32, above, 1)
@@ -667,7 +676,7 @@
         slot_near.append(jnp.where(near_columns == column, near_at, -1))
         slot_far.append(jnp.where(far_columns == column, far_at, -1))
     code = jnp.full(above, -1, jnp.int32)
-    for j in range(2 * r_slots):
+    for j in range(both):
         block = my_low if j < r_slots else my_high
         named = block[:, j % r_slots : j % r_slots + 1]
         in_own = own_fine == named
@@ -678,184 +687,244 @@
             found = jnp.where(in_near, slot_near[index], found)
             found = jnp.where(in_far, slot_far[index], found)
             best = jnp.max(found, axis=1, keepdims=True)
-            code = jnp.where(table_lanes == index * 2 * r_slots + j, best, code)
+            code = jnp.where(table_lanes == index * both + j, best, code)
     tables[0:row_count, :] = jnp.where((code >= 0) & (code < REMOTE), code, zero_own)
-    tables[row_count : 2 * row_count, :] = jnp.where(code >= REMOTE, code - REMOTE, zero_near)
+    away = code >= REMOTE
+    rank = away.astype(jnp.int32)
+    table_j = lax.rem(table_lanes, both)
+    step = 1
+    while step < both:
+        rank = rank + jnp.where(table_j >= step, pltpu.roll(rank, step, 1), 0)
+        step *= 2
+    crowded = jnp.max(jnp.max(rank, axis=1, keepdims=True), axis=0, keepdims=True)
+    job = jnp.where(away, (code - REMOTE) * both + table_j, -1)
+    rank = jnp.where(away, rank - 1 + (table_lanes // both) * JOBS, -1)
+    short = jnp.full(above, -1, jnp.int32)
+    for at in range(half_cap * JOBS):
+        best = jnp.max(jnp.where(rank == at, job, -1), axis=1, keepdims=True)
+        short = jnp.where(table_lanes == at, best, short)
+    job_j = lax.rem(jnp.maximum(short, 0), both)
+    job_c = lax.broadcasted_iota(jnp.int32, above, 0)
+    job_r = (job_j // r_slots) * (row_count * r_slots) + job_c * r_slots + lax.rem(job_j, r_slots)
+    tables[row_count : 2 * row_count, :] = jnp.where(short >= 0, short // both, zero_near)
+    tables[2 * row_count : 3 * row_count, :] = job_r
     code_copy = pltpu.make_async_copy(tables, codes, table_sems.at[1])
     code_copy.start()
 
-    def earlier(index, total):
-        block = gathered[index * groups]
-        return total + jnp.sum(block[:, live : live + 1], axis=0, keepdims=True)
-
-    first = lax.fori_loop(0, row, earlier, jnp.zeros((1, 1), jnp.int32))
-    counts = jnp.broadcast_to(own_counts, small)
-    inner_sum = jnp.sum(
-        jnp.where(
-            lax.broadcasted_iota(jnp.int32, small, 0) < lax.broadcasted_iota(jnp.int32, small, 1),
-            counts, 0,
-        ),
-        axis=0, keepdims=True,
+    over = jnp.maximum(near_total - 2 * list_slots, far_total - 2 * pass_slots)
+    over = jnp.maximum(over, crowded - JOBS)
+    over = (over > 0).astype(jnp.int32)
+    told[group] = jnp.broadcast_to(over, told.shape[1:])
+
+    def tell(ahead):
+        return remote(
+            told.at[group], told.at[group], told_sems.at[0], told_sems.at[1],
+            (row, lax.rem(group + ahead, groups)),
+        )
+
+    for ahead in range(1, groups):
+        tell(ahead).start()
+
+    tile = pair_a.shape[1]
+    total_count = jnp.sum(own_counts, axis=0, keepdims=True)
+
+    def scan_copy(k, side):
+        other = row + (1 << k) if side == 0 else row - (1 << k)
+        return remote(
+            scan_out.at[k], scan_in.at[k, side], scan_sems.at[0, k, side], scan_sems.at[1, k, side],
+            (other, group),
+        )
+
+    scan_shape = scan_out.shape[1:]
+    scan_lane = lax.broadcasted_iota(jnp.int32, scan_shape, 1)
+    above_there = [row + (1 << k) < rows for k in range(rounds)]
+    below_there = [row - (1 << k) >= 0 for k in range(rounds)]
+
+    def scan_send(k, state):
+        scan_out[k] = state
+
+        @pl.when(above_there[k])
+        def _():
+            scan_copy(k, 0).start()
+
+        @pl.when(below_there[k])
+        def _():
+            scan_copy(k, 1).start()
+
+    def scan_take(k, state):
+        @pl.when(below_there[k])
+        def _():
+            scan_copy(k, 0).wait_recv()
+
+        @pl.when(above_there[k])
+        def _():
+            scan_copy(k, 1).wait_recv()
+
+        below = jnp.where((scan_lane < 2) & below_there[k], scan_in[k, 0], 0)
+        beyond = jnp.where((scan_lane == 2) & above_there[k], scan_in[k, 1], 0)
+        return state + below + beyond
+
+    wait_bytes(told.at[pl.ds(0, groups - 1)], told_sems.at[1])
+    over = told[0]
+    for other_group in range(1, groups):
+        over = over + told[other_group]
+    state = jnp.where(
+        scan_lane == 0, jnp.broadcast_to(total_count, scan_shape),
+        jnp.where(scan_lane < 3, over, 0),
     )
-    offsets_ref[...] = inner_sum + first
+    scan_send(0, state)
+
+    def mate_copy(view, sems):
+        return remote(view, view, sems.at[0], sems.at[1], mate_place)
+
+    early_view = landed.at[pl.ds(part * near_slots, early)]
+    early_far_view = landed.at[pl.ds(far_base + part * far_slots, early)]
+
+    def far_view(index):
+        return landed.at[pl.ds(far_base + part * far_slots + early + index * chunk, chunk)]
+
+    early_far = remote(early_view, early_far_view, far_send.at[0], far_sems.at[far_chunks], (onward, group))
+
+    def far_copy(index):
+        return remote(
+            near_view(index), far_view(index), far_send.at[0], far_sems.at[index], (onward, group)
+        )
+
+    def take_far(index):
+        @pl.when(has_far)
+        def _():
+            if index < 0:
+                early_far.wait_recv()
+                mate_copy(early_far_view, far_pair_sems).start()
+            else:
+                far_copy(index).wait_recv()
+                mate_copy(far_view(index), far_pair_sems).start()
+
+    early_copy.wait_recv()
+
+    @pl.when(has_onward)
+    def _():
+        early_far.start()
+
+    mate_copy(early_view, near_pair_sems).start()
     code_copy.wait()
     own_r.wait()
     mate_r.wait_recv()
 
-    tile = pair_a.shape[1:]
-
-    def multiply(c, stage, index, source):
-        total = None
-        for j in range(0, 2 * r_slots, 2):
-            left = jnp.concatenate(
-                [pair_r[x // r_slots, c * r_slots + x % r_slots] for x in (j, j + 1)], axis=1
-            )
-            right = jnp.concatenate(
-                [
-                    jnp.concatenate(
-                        [
-                            source[codes[stage * row_count + c, slot * 2 * r_slots + x]]
-                            for slot in (index, index + 1)
-                        ],
-                        axis=1,
-                    )
-                    for x in (j, j + 1)
-                ],
-                axis=0,
-            )
-            term = jnp.dot(left, right, preferred_element_type=jnp.float32)
-            total = term if total is None else total + term
-        return total
+    def flat_r(index):
+        return pair_r[index // (row_count * r_slots), lax.rem(index, row_count * r_slots)]
 
     def own_stage(c, carry):
         for index in range(0, half_cap, 2):
-            sums[c * half_cap // 2 + index // 2] = multiply(c, 0, index, pair_a)
+            total = None
+            for j in range(0, both, 2):
+                left = jnp.concatenate(
+                    [pair_r[x // r_slots, c * r_slots + x % r_slots] for x in (j, j + 1)], axis=1
+                )
+                right = jnp.concatenate(
+                    [
+                        jnp.concatenate(
+                            [pair_a[codes[c, slot * both + x]] for slot in (index, index + 1)], axis=1
+                        )
+                        for x in (j, j + 1)
+                    ],
+                    axis=0,
+                )
+                term = jnp.dot(left, right, preferred_element_type=jnp.float32)
+                total = term if total is None else total + term
+            sums[c * half_cap + index] = total[:, :tile]
+            sums[c * half_cap + index + 1] = total[:, tile:]
         return carry
 
-    lax.fori_loop(0, row_count, own_stage, 0)
-
-    def near_mate(index):
-        view = landed.at[pl.ds(part * near_slots + index * chunk, chunk)]
-        return remote(view, view, near_pair_sems.at[0, index], near_pair_sems.at[1, index], mate_place)
-
-    def far_view(index):
-        return landed.at[pl.ds(far_base + part * far_slots + index * chunk, chunk)]
-
-    def far_copy(index):
-        return remote(
-            landed.at[pl.ds(part * near_slots + index * chunk, chunk)], far_view(index),
-            far_sems.at[0, index], far_sems.at[1, index], (onward, group),
-        )
-
-    def far_mate(index):
-        view = far_view(index)
-        return remote(
-            view, view, far_pair_sems.at[0, index], far_pair_sems.at[1, index], mate_place
-        )
-
-    def take_far(index):
-        @pl.when(has_far)
-        def _():
-            far_copy(index).wait_recv()
-            far_mate(index).start()
-
     lag = 2
+    scans = 0
     for index in range(near_chunks):
         near_copy(index).wait_recv()
         if index < far_chunks:
             @pl.when(has_onward)
             def _():
                 far_copy(index).start()
-        near_mate(index).start()
-        if 0 <= index - lag < far_chunks:
+        mate_copy(near_view(index), near_pair_sems).start()
+        if -1 <= index - lag < far_chunks:
             take_far(index - lag)
-    for index in range(max(near_chunks - lag, 0), far_chunks):
+        lax.fori_loop(
+            index * row_count // near_chunks, (index + 1) * row_count // near_chunks, own_stage, 0
+        )
+        if index > 0 and scans < rounds:
+            state = scan_take(scans, state)
+            scans += 1
+            if scans < rounds:
+                scan_send(scans, state)
+    for index in range(max(near_chunks - lag, -1), far_chunks):
         take_far(index)
-
-    pair_count = rows * pairs
-
-    def crowd(which, most):
-        which_row = which // pairs
-        base_group = 2 * lax.rem(which, pairs)
-        parity = lax.rem(which_row, 2)
-        which_near = which_row + 1 - 2 * parity
-        which_far = which_row - 1 + 2 * parity
-        far_there = (which_far >= 0) & (which_far < rows)
-        start = (which_row * groups + base_group) * local_rows
-        columns = pair_columns_at(start)
-        fine = lane_fine + start
-        near_base = which_near * groups + base_group
-        far_base_at = jnp.clip(which_far, 0, rows - 1) * groups + base_group
-        by_near = need_of(gathered[near_base], gathered[near_base + 1], columns, fine)
-        by_far = need_of(gathered[far_base_at], gathered[far_base_at + 1], columns, fine)
-        by_far = jnp.where(far_there, by_far, 0)
-        sends = jnp.sum(jnp.maximum(by_near, by_far), axis=1, keepdims=True)
-        passes = jnp.sum(by_far, axis=1, keepdims=True)
-        over = jnp.maximum(sends - 2 * near_slots, passes - 2 * far_slots)
-        return jnp.maximum(most, over)
-
-    worst_over = lax.fori_loop(0, pair_count, crowd, jnp.full((1, 1), -1, jnp.int32))
-    flag_ref[...] = (worst_over > 0).astype(jnp.int32)
-
-    for index in range(near_chunks):
-        near_mate(index).wait_recv()
+    while scans < rounds:
+        state = scan_take(scans, state)
+        scans += 1
+        if scans < rounds:
+            scan_send(scans, state)
+
+    flags = jnp.where((scan_lane == 1) | (scan_lane == 2), state, 0)
+    flags = jnp.max(jnp.max(flags, axis=1, keepdims=True), axis=0, keepdims=True)
+    flag_ref[...] = (flags > 0).astype(jnp.int32)
+    reached = jnp.where(scan_lane == 0, state, 0)
+    reached = jnp.max(jnp.max(reached, axis=1, keepdims=True), axis=0, keepdims=True)
+    earlier = lax.broadcasted_iota(jnp.int32, small, 0) < lax.broadcasted_iota(jnp.int32, small, 1)
+    counts = jnp.broadcast_to(own_counts, small)
+    inner_sum = jnp.sum(jnp.where(earlier, counts, 0), axis=0, keepdims=True)
+    offsets_ref[...] = inner_sum + (reached - total_count)
+
+    wait_bytes(landed.at[pl.ds(0, near_slots)], near_pair_sems.at[1])
 
     @pl.when(has_far)
     def _():
-        for index in range(far_chunks):
-            far_mate(index).wait_recv()
+        wait_bytes(landed.at[pl.ds(0, far_slots)], far_pair_sems.at[1])
 
     ahead_of = [lax.rem(index // own_cap + pairs - group // 2, pairs) for index in range(half_cap)]
 
-    def out_copy(c, index):
-        return pltpu.make_async_copy(
-            done.at[c * half_cap + index],
-            out_ref.at[ahead_of[index] * row_count * own_cap + c * own_cap + index % own_cap],
-            out_sems.at[c * half_cap + index],
-        )
-
     def near_stage(c, carry):
-        for index in range(0, half_cap, 2):
-            total = sums[c * half_cap // 2 + index // 2] + multiply(c, 1, index, landed)
-            total = total.astype(done.dtype)
-            done[c * half_cap + index] = total[:, : tile[1]]
-            done[c * half_cap + index + 1] = total[:, tile[1] :]
         for index in range(half_cap):
-            out_copy(c, index).start()
+            total = sums[c * half_cap + index]
+            for at in range(index * JOBS, (index + 1) * JOBS, 2):
+                left = jnp.concatenate(
+                    [flat_r(codes[2 * row_count + c, x]) for x in (at, at + 1)], axis=1
+                )
+                right = jnp.concatenate(
+                    [landed[codes[row_count + c, x]] for x in (at, at + 1)], axis=0
+                )
+                total = total + jnp.dot(left, right, preferred_element_type=jnp.float32)
+            place = ahead_of[index] * row_count * own_cap + c * own_cap + index % own_cap
+            out_ref[place] = total.astype(out_ref.dtype)
         return carry
 
     lax.fori_loop(0, row_count, near_stage, 0)
 
-    sent = gathered.at[pl.ds(0, count - 1)]
-    pltpu.make_async_copy(sent, sent, gather_sems.at[0]).wait()
-    wait_close_send(0)
-
-    @pl.when(has_far)
-    def _():
-        wait_close_send(2)
-
+    wait_bytes(close.at[pl.ds(0, 2)], close_sems.at[0, 0])
+    to_mate.wait_send()
     mate_a.wait_send()
     mate_r.wait_send()
-    for index in range(near_chunks):
-        near_copy(index).wait_send()
-        near_mate(index).wait_send()
+    early_copy.wait_send()
+    place_copy.wait_send()
+    wait_bytes(packed, near_send.at[0])
+    wait_bytes(told.at[pl.ds(0, groups - 1)], told_sems.at[0])
+    wait_bytes(landed.at[pl.ds(0, near_slots)], near_pair_sems.at[0])
 
     @pl.when(has_onward)
     def _():
-        for index in range(far_chunks):
-            far_copy(index).wait_send()
+        wait_bytes(landed.at[pl.ds(0, far_slots)], far_send.at[0])
 
     @pl.when(has_far)
     def _():
-        for index in range(far_chunks):
-            far_mate(index).wait_send()
-
-    def finish(c, carry):
-        for index in range(half_cap):
-            out_copy(c, index).wait()
-        return carry
-
-    lax.fori_loop(0, row_count, finish, 0)
+        wait_bytes(close.at[pl.ds(2, 2)], close_sems.at[0, 1])
+        wait_bytes(landed.at[pl.ds(0, far_slots)], far_pair_sems.at[0])
+
+    for k in range(rounds):
+        @pl.when(above_there[k])
+        def _():
+            scan_copy(k, 0).wait_send()
+
+        @pl.when(below_there[k])
+        def _():
+            scan_copy(k, 1).wait_send()
 
 
 def pair_sum_kernel(pairs, own, part_ref, landed, send_sems, recv_sems):
@@ -892,21 +961,24 @@
     cap = c_cols.shape[1]
     tiles = local_rows * op_slots
     pairs = groups // 2
-    count = rows * groups
     own_cap = cap // groups
     half_cap = cap // 2
     width = -(-2 * tiles // 128) * 128
-    near_slots = min(NEAR_SLOTS, -(-tiles // CHUNK) * CHUNK)
-    far_slots = min(FAR_SLOTS, near_slots)
-    dims = (rows, groups, local_rows, op_slots, r_slots, cap, width, near_slots, far_slots, CHUNK)
-    near_chunks = near_slots // CHUNK
-    far_chunks = far_slots // CHUNK
+    list_slots = min(LIST_SLOTS, -(-tiles // CHUNK) * CHUNK)
+    pass_slots = min(PASS_SLOTS, list_slots)
+    dims = (rows, groups, local_rows, op_slots, r_slots, cap, width, list_slots, pass_slots, CHUNK)
+    near_chunks = list_slots // CHUNK
+    far_chunks = pass_slots // CHUNK
+    near_slots = op_slots + list_slots
+    far_slots = op_slots + pass_slots
+    rounds = (rows - 1).bit_length()
     dtype = a_tiles.dtype
     out_dtype = jnp.bfloat16 if pairs == 1 else jnp.float32
     own = row_count * own_cap
     vmem = pl.BlockSpec(memory_space=pltpu.VMEM)
     anywhere = pl.BlockSpec(memory_space=pl.ANY)
     dma = pltpu.SemaphoreType.DMA
+    block = (row_count, 128)
     part, offsets, flag = pl.pallas_call(
         functools.partial(fused_kernel, dims),
         out_shape=(
@@ -914,31 +986,41 @@
             jax.ShapeDtypeStruct((1, row_count), jnp.int32),
             jax.ShapeDtypeStruct((1, 1), jnp.int32),
         ),
-        in_specs=[vmem] * 4 + [anywhere] * 2,
-        out_specs=(anywhere, vmem, vmem),
+        in_specs=[anywhere] * 6,
+        out_specs=(vmem, vmem, vmem),
         scratch_shapes=[
-            pltpu.VMEM((row_count, 128), jnp.int32),
-            pltpu.VMEM((count, row_count, 128), jnp.int32),
-            pltpu.VMEM((4, row_count, 128), jnp.int32),
+            pltpu.VMEM(r_cols.shape, jnp.int32),
+            pltpu.VMEM(c_cols.shape, jnp.int32),
+            pltpu.VMEM((1, row_count), jnp.int32),
+            pltpu.VMEM((op_slots, a_cols.shape[0]), jnp.int32),
+            pltpu.VMEM(block, jnp.int32),
+            pltpu.VMEM((5,) + block, jnp.int32),
+            pltpu.VMEM((2, 8, width), jnp.int32),
             pltpu.VMEM((2 * tiles + 1, tile, tile), dtype),
             pltpu.VMEM((2, row_count * r_slots, tile, tile), dtype),
-            pltpu.VMEM((near_slots, tile, tile), dtype),
+            pltpu.VMEM((list_slots, tile, tile), dtype),
             pltpu.VMEM((2 * (near_slots + far_slots) + 1, tile, tile), dtype),
-            pltpu.VMEM((row_count * half_cap // 2, tile, 2 * tile), jnp.float32),
-            pltpu.VMEM((row_count * half_cap, tile, tile), out_dtype),
-            pltpu.VMEM((2 * row_count, width), jnp.int32),
-            pltpu.SMEM((2 * row_count, width), jnp.int32),
+            pltpu.VMEM((row_count * half_cap, tile, tile), jnp.float32),
+            pltpu.VMEM((3 * row_count, width), jnp.int32),
+            pltpu.SMEM((3 * row_count, width), jnp.int32),
             pltpu.SMEM((8, width), jnp.int32),
+            pltpu.VMEM((groups, 8, 128), jnp.int32),
+            pltpu.VMEM((rounds, 8, 128), jnp.int32),
+            pltpu.VMEM((rounds, 2, 8, 128), jnp.int32),
+            dma((6,)),
+            dma((2, 3)),
+            dma((2, 2)),
             dma((2,)),
             dma((2,)),
-            dma((2, 4)),
-            dma((2, 2)),
-            dma((2, near_chunks)),
-            dma((2, near_chunks)),
-            dma((2, far_chunks)),
-            dma((2, far_chunks)),
+            dma((near_chunks,)),
+            dma((1,)),
             dma((2,)),
-            dma((row_count * half_cap,)),
+            dma((far_chunks + 1,)),
+            dma((1,)),
+            dma((2,)),
+            dma((2,)),
+            dma((2,)),
+            dma((2, rounds, 2)),
         ],
         compiler_params=pltpu.CompilerParams(collective_id=40, has_side_effects=True),
         name="fused",

time: 49.2 us -> 50.3 us (1.022)
  Pallas kernels: 46.1 us -> 46.9 us
    pallas_call x1, Pallas kernels: 46.1 us -> 46.9 us  [fused_body(): pl.pallas_call(functools.partial(fused_kernel, dims), out_shape=(jax.Shap...]
where the time goes in v1:
time: 50.3 us; the launch traced here: 49.8 us
  Pallas kernels  46.9 us (93%)
  local copies, waits for them, and re-layouts  1.5 us (3%)
  between operations  1.4 us (3%)
    pallas_call x1, Pallas kernels, fused_body(): pl.pallas_call(functools.partial(fused_kernel, dims), out_shape=(jax.Shap...  46.9 us
    unnamed x12, local copies, waits for them, and re-layouts  1.5 us

profile of v1, /device:TPU:0, one launch (start us, length us, event | category | flops | bytes accessed | tf_op | source)
XLA Modules:
  0.0 49.8 jit_solution(3255953203922367750)
XLA Ops:
  0.6 0.0 copy-start.4
  0.6 0.0 copy-start.3
  0.7 0.0 copy-start.2
  0.7 0.0 copy-start
  0.7 0.0 copy-start.1
  0.7 46.9 %fused.1 = (bf16[32,128,128]{2,1,0:T(8,128)(2,1)S(1)}, s32[1,8]{1,0:T(1,128)S(1)}, s32[1,1]{1,0:T(1,128)}) custom-call(s32[8,8]{1,0:T(8,128)} %r_cols_hbm.1, s32[8,8]{1,0:T(8,128)} %c_cols_hbm.1, s32[1,8]{1,0:T(1,128)} %bitcast.74, s32[7,256]{1,0:T(8,128)} %bitcast.73, bf16[56,128,128]{2,1,0:T(8,128)(2,1)} %bitcast.33, bf16[64,128,128]{2,1,0:T(8,128)(2,1)} %bitcast.69), custom_call_target="tpu_custom_call" | custom-call | tf_op jit(solution)/shard_map/fused/pallas_call | solution.py:982
  48.3 0.0 copy-done.4
  48.3 0.0 copy-done.3
  48.3 0.0 copy-done.2
  48.3 0.0 copy-done
  48.3 0.0 copy-done.1
  48.3 1.0 %copy.33 = bf16[8,4,128,128]{3,2,1,0:T(8,128)(2,1)} copy(bf16[8,4,128,128]{3,2,1,0:T(8,128)(2,1)S(1)} %get-tuple-element.183) | data formatting | bytes 2097152
  49.3 0.5 %copy.34 = s32[8]{0:T(128)} copy(s32[8]{0:T(128)S(1)} %get-tuple-element.184) | data formatting | bytes 64
  (1 shorter events, 0.0 us)
Async XLA Ops:
  0.6 47.7 %copy-start.4 = (s32[8]{0:T(128)S(1)}, s32[8]{0:T(128)}, u32[]{:S(2)}) copy-start(s32[8]{0:T(128)} %param.30) | copy-start | bytes 100
  0.6 47.7 %copy-start.3 = (s32[8,8]{1,0:T(8,128)S(1)}, s32[8,8]{1,0:T(8,128)}, u32[]{:S(2)}) copy-start(s32[8,8]{1,0:T(8,128)} %c_cols_hbm.1) | copy-start | bytes 772
  0.7 47.7 %copy-start.2 = (s32[256,7]{0,1:T(8,128)S(1)}, s32[256,7]{0,1:T(8,128)}, u32[]{:S(2)}) copy-start(s32[256,7]{0,1:T(8,128)} %param.28) | copy-start | bytes 21508
  0.7 47.7 %copy-start = (bf16[8,7,128,128]{3,2,1,0:T(8,128)(2,1)S(1)}, bf16[8,7,128,128]{3,2,1,0:T(8,128)(2,1)}, u32[]{:S(2)}) copy-start(bf16[8,7,128,128]{3,2,1,0:T(8,128)(2,1)} %param.27) | copy-start | bytes 5505028
  0.7 47.7 %copy-start.1 = (s32[8,8]{1,0:T(8,128)S(1)}, s32[8,8]{1,0:T(8,128)}, u32[]{:S(2)}) copy-start(s32[8,8]{1,0:T(8,128)} %r_cols_hbm.1) | copy-start | bytes 772

commit v2 on v1

--- a/solution.py
+++ b/solution.py
@@ -436,6 +436,7 @@
     zero_near = 2 * (near_slots + far_slots)
     zero_own = 2 * tiles
     rounds = (rows - 1).bit_length()
+    order = [*range(1, rounds), 0]
 
     row = lax.axis_index("rows")
     group = lax.axis_index("inner")
@@ -482,7 +483,7 @@
     own_a = pltpu.make_async_copy(
         a_ref, pair_a.at[pl.ds(part * tiles, tiles)], local_sems.at[0]
     )
-    own_r = pltpu.make_async_copy(r_ref, pair_r.at[part], local_sems.at[1])
+    own_r = pltpu.make_async_copy(r_ref, pair_r.at[pl.ds(part * row_count * r_slots, row_count * r_slots)], local_sems.at[1])
     own_a.start()
     own_r.start()
 
@@ -506,8 +507,6 @@
     own_counts = jnp.sum(jnp.where(diagonal, spread_counts, 0), axis=1, keepdims=True)
     meta[:, 0:r_slots] = r_cols_ref[...]
     meta[:, r_slots:live] = c_cols_ref[...]
-    own_a.wait()
-
     pl.semaphore_wait(barrier, groups + 1 + 2 * has_far.astype(jnp.int32))
 
     def start_close(target, first, which):
@@ -529,12 +528,13 @@
     )
     mate_a.start()
 
+    own_a.wait()
     early_copy = remote(
         pair_a.at[pl.ds(part * tiles, early)], landed.at[pl.ds(part * near_slots, early)],
         early_sems.at[0], early_sems.at[1], (near, group),
     )
     early_copy.start()
-    mate_r = remote(r_ref, pair_r.at[part], pair_sems.at[0, 1], pair_sems.at[1, 1], mate_place)
+    mate_r = remote(r_ref, pair_r.at[pl.ds(part * row_count * r_slots, row_count * r_slots)], pair_sems.at[0, 1], pair_sems.at[1, 1], mate_place)
     mate_r.start()
 
     lanes = lax.broadcasted_iota(jnp.int32, (1, width), 1)
@@ -648,11 +648,44 @@
             pack(index + 1)
         near_copy(index).start()
 
+    def mate_copy(view, sems):
+        return remote(view, view, sems.at[0], sems.at[1], mate_place)
+
+    early_view = landed.at[pl.ds(part * near_slots, early)]
+    early_far_view = landed.at[pl.ds(far_base + part * far_slots, early)]
+
+    def far_view(index):
+        return landed.at[pl.ds(far_base + part * far_slots + early + index * chunk, chunk)]
+
+    early_far = remote(early_view, early_far_view, far_send.at[0], far_sems.at[far_chunks], (onward, group))
+
+    def far_copy(index):
+        return remote(
+            near_view(index), far_view(index), far_send.at[0], far_sems.at[index], (onward, group)
+        )
+
+    def take_far(index):
+        @pl.when(has_far)
+        def _():
+            if index < 0:
+                early_far.wait_recv()
+                mate_copy(early_far_view, far_pair_sems).start()
+            else:
+                far_copy(index).wait_recv()
+                mate_copy(far_view(index), far_pair_sems).start()
+
     near_columns = pair_columns(near)
     near_fine = pair_fine(near)
     far_row = jnp.clip(far, 0, rows - 1)
     far_columns = pair_columns(far_row)
     far_fine = jnp.where(has_far, pair_fine(far_row), -(1 << 24))
+    early_copy.wait_recv()
+
+    @pl.when(has_onward)
+    def _():
+        early_far.start()
+
+    mate_copy(early_view, near_pair_sems).start()
     to_mate.wait_recv()
     mine, other = meta[...], close[4]
     my_low = jnp.where(part == 0, mine, other)
@@ -772,54 +805,18 @@
         scan_lane == 0, jnp.broadcast_to(total_count, scan_shape),
         jnp.where(scan_lane < 3, over, 0),
     )
-    scan_send(0, state)
-
-    def mate_copy(view, sems):
-        return remote(view, view, sems.at[0], sems.at[1], mate_place)
-
-    early_view = landed.at[pl.ds(part * near_slots, early)]
-    early_far_view = landed.at[pl.ds(far_base + part * far_slots, early)]
-
-    def far_view(index):
-        return landed.at[pl.ds(far_base + part * far_slots + early + index * chunk, chunk)]
-
-    early_far = remote(early_view, early_far_view, far_send.at[0], far_sems.at[far_chunks], (onward, group))
-
-    def far_copy(index):
-        return remote(
-            near_view(index), far_view(index), far_send.at[0], far_sems.at[index], (onward, group)
-        )
-
-    def take_far(index):
-        @pl.when(has_far)
-        def _():
-            if index < 0:
-                early_far.wait_recv()
-                mate_copy(early_far_view, far_pair_sems).start()
-            else:
-                far_copy(index).wait_recv()
-                mate_copy(far_view(index), far_pair_sems).start()
-
-    early_copy.wait_recv()
-
-    @pl.when(has_onward)
-    def _():
-        early_far.start()
-
-    mate_copy(early_view, near_pair_sems).start()
+    scan_send(order[0], state)
+
     code_copy.wait()
     own_r.wait()
     mate_r.wait_recv()
-
-    def flat_r(index):
-        return pair_r[index // (row_count * r_slots), lax.rem(index, row_count * r_slots)]
 
     def own_stage(c, carry):
         for index in range(0, half_cap, 2):
             total = None
             for j in range(0, both, 2):
                 left = jnp.concatenate(
-                    [pair_r[x // r_slots, c * r_slots + x % r_slots] for x in (j, j + 1)], axis=1
+                    [pair_r[x // r_slots * row_count * r_slots + c * r_slots + x % r_slots] for x in (j, j + 1)], axis=1
                 )
                 right = jnp.concatenate(
                     [
@@ -836,7 +833,7 @@
             sums[c * half_cap + index + 1] = total[:, tile:]
         return carry
 
-    lag = 2
+    lag = 3
     scans = 0
     for index in range(near_chunks):
         near_copy(index).wait_recv()
@@ -850,18 +847,17 @@
         lax.fori_loop(
             index * row_count // near_chunks, (index + 1) * row_count // near_chunks, own_stage, 0
         )
-        if index > 0 and scans < rounds:
-            state = scan_take(scans, state)
+        if index > 0 and scans < rounds - 1:
+            state = scan_take(order[scans], state)
             scans += 1
-            if scans < rounds:
-                scan_send(scans, state)
+            scan_send(order[scans], state)
     for index in range(max(near_chunks - lag, -1), far_chunks):
         take_far(index)
     while scans < rounds:
-        state = scan_take(scans, state)
+        state = scan_take(order[scans], state)
         scans += 1
         if scans < rounds:
-            scan_send(scans, state)
+            scan_send(order[scans], state)
 
     flags = jnp.where((scan_lane == 1) | (scan_lane == 2), state, 0)
     flags = jnp.max(jnp.max(flags, axis=1, keepdims=True), axis=0, keepdims=True)
@@ -883,15 +879,12 @@
 
     def near_stage(c, carry):
         for index in range(half_cap):
-            total = sums[c * half_cap + index]
-            for at in range(index * JOBS, (index + 1) * JOBS, 2):
-                left = jnp.concatenate(
-                    [flat_r(codes[2 * row_count + c, x]) for x in (at, at + 1)], axis=1
-                )
-                right = jnp.concatenate(
-                    [landed[codes[row_count + c, x]] for x in (at, at + 1)], axis=0
-                )
-                total = total + jnp.dot(left, right, preferred_element_type=jnp.float32)
+            jobs = range(index * JOBS, (index + 1) * JOBS)
+            left = jnp.concatenate([pair_r[codes[2 * row_count + c, x]] for x in jobs], axis=1)
+            right = jnp.concatenate([landed[codes[row_count + c, x]] for x in jobs], axis=0)
+            total = sums[c * half_cap + index] + jnp.dot(
+                left, right, preferred_element_type=jnp.float32
+            )
             place = ahead_of[index] * row_count * own_cap + c * own_cap + index % own_cap
             out_ref[place] = total.astype(out_ref.dtype)
         return carry
@@ -997,7 +990,7 @@
             pltpu.VMEM((5,) + block, jnp.int32),
             pltpu.VMEM((2, 8, width), jnp.int32),
             pltpu.VMEM((2 * tiles + 1, tile, tile), dtype),
-            pltpu.VMEM((2, row_count * r_slots, tile, tile), dtype),
+            pltpu.VMEM((2 * row_count * r_slots, tile, tile), dtype),
             pltpu.VMEM((list_slots, tile, tile), dtype),
             pltpu.VMEM((2 * (near_slots + far_slots) + 1, tile, tile), dtype),
             pltpu.VMEM((row_count * half_cap, tile, tile), jnp.float32),

time: 50.3 us -> 37.9 us (0.75)
  Pallas kernels: 46.9 us -> 34.6 us
    pallas_call x1, Pallas kernels: 46.9 us -> 34.6 us  [fused_body(): pl.pallas_call(functools.partial(fused_kernel, dims), out_shape=(jax.Shap...]
where the time goes in v2:
time: 37.9 us; the launch traced here: 37.5 us
  Pallas kernels  34.6 us (91%)
  local copies, waits for them, and re-layouts  1.5 us (4%)
  between operations  1.4 us (4%)
    pallas_call x1, Pallas kernels, fused_body(): pl.pallas_call(functools.partial(fused_kernel, dims), out_shape=(jax.Shap...  34.6 us
    unnamed x12, local copies, waits for them, and re-layouts  1.5 us

profile of v2, /device:TPU:0, one launch (start us, length us, event | category | flops | bytes accessed | tf_op | source)
XLA Modules:
  0.0 37.5 jit_solution(448208324517163415)
XLA Ops:
  0.6 0.0 copy-start.4
  0.6 0.0 copy-start.3
  0.7 0.0 copy-start.2
  0.7 0.0 copy-start
  0.7 0.0 copy-start.1
  0.7 34.6 %fused.1 = (bf16[32,128,128]{2,1,0:T(8,128)(2,1)S(1)}, s32[1,8]{1,0:T(1,128)S(1)}, s32[1,1]{1,0:T(1,128)}) custom-call(s32[8,8]{1,0:T(8,128)} %r_cols_hbm.1, s32[8,8]{1,0:T(8,128)} %c_cols_hbm.1, s32[1,8]{1,0:T(1,128)} %bitcast.74, s32[7,256]{1,0:T(8,128)} %bitcast.73, bf16[56,128,128]{2,1,0:T(8,128)(2,1)} %bitcast.33, bf16[64,128,128]{2,1,0:T(8,128)(2,1)} %bitcast.69), custom_call_target="tpu_custom_call" | custom-call | tf_op jit(solution)/shard_map/fused/pallas_call | solution.py:975
  36.0 0.0 copy-done.4
  36.0 0.0 copy-done.3
  36.0 0.0 copy-done.2
  36.0 0.0 copy-done
  36.0 0.0 copy-done.1
  36.0 1.0 %copy.33 = bf16[8,4,128,128]{3,2,1,0:T(8,128)(2,1)} copy(bf16[8,4,128,128]{3,2,1,0:T(8,128)(2,1)S(1)} %get-tuple-element.183) | data formatting | bytes 2097152
  37.0 0.5 %copy.34 = s32[8]{0:T(128)} copy(s32[8]{0:T(128)S(1)} %get-tuple-element.184) | data formatting | bytes 64
  (1 shorter events, 0.0 us)
Async XLA Ops:
  0.6 35.4 %copy-start.4 = (s32[8]{0:T(128)S(1)}, s32[8]{0:T(128)}, u32[]{:S(2)}) copy-start(s32[8]{0:T(128)} %param.30) | copy-start | bytes 100
  0.6 35.4 %copy-start.3 = (s32[8,8]{1,0:T(8,128)S(1)}, s32[8,8]{1,0:T(8,128)}, u32[]{:S(2)}) copy-start(s32[8,8]{1,0:T(8,128)} %c_cols_hbm.1) | copy-start | bytes 772
  0.7 35.4 %copy-start.2 = (s32[256,7]{0,1:T(8,128)S(1)}, s32[256,7]{0,1:T(8,128)}, u32[]{:S(2)}) copy-start(s32[256,7]{0,1:T(8,128)} %param.28) | copy-start | bytes 21508
  0.7 35.4 %copy-start = (bf16[8,7,128,128]{3,2,1,0:T(8,128)(2,1)S(1)}, bf16[8,7,128,128]{3,2,1,0:T(8,128)(2,1)}, u32[]{:S(2)}) copy-start(bf16[8,7,128,128]{3,2,1,0:T(8,128)(2,1)} %param.27) | copy-start | bytes 5505028
  0.7 35.4 %copy-start.1 = (s32[8,8]{1,0:T(8,128)S(1)}, s32[8,8]{1,0:T(8,128)}, u32[]{:S(2)}) copy-start(s32[8,8]{1,0:T(8,128)} %r_cols_hbm.1) | copy-start | bytes 772

commit v3 on v2

--- a/solution.py
+++ b/solution.py
@@ -405,7 +405,7 @@
 LIST_SLOTS = 27
 PASS_SLOTS = 15
 CHUNK = 3
-JOBS = 6
+JOBS = 4
 REMOTE = 1 << 14
 
 
@@ -436,7 +436,6 @@
     zero_near = 2 * (near_slots + far_slots)
     zero_own = 2 * tiles
     rounds = (rows - 1).bit_length()
-    order = [*range(1, rounds), 0]
 
     row = lax.axis_index("rows")
     group = lax.axis_index("inner")
@@ -562,12 +561,16 @@
     def pair_fine(which_row):
         return lane_fine + (which_row * groups + first_group) * local_rows
 
-    def need_of(meta_low, meta_high, columns, fine):
+    def named_by(meta_low, meta_high, fine):
         named = fine == meta_low[:, 0:1]
         for j in range(1, r_slots):
             named = named | (fine == meta_low[:, j : j + 1])
         for j in range(r_slots):
             named = named | (fine == meta_high[:, j : j + 1])
+        return named
+
+    def need_of(meta_low, meta_high, columns, fine):
+        named = named_by(meta_low, meta_high, fine)
         wanted = columns == meta_low[:, r_slots : r_slots + 1]
         for s in range(1, cap):
             wanted = wanted | (columns == meta_low[:, r_slots + s : r_slots + s + 1])
@@ -626,6 +629,96 @@
     placing[0] = jnp.broadcast_to(landing(places, list_slots, 0, near_slots), placing.shape[1:])
     place_copy = remote(placing.at[0], placing.at[1], place_sems.at[0], place_sems.at[1], (near, group))
     place_copy.start()
+    near_columns = pair_columns(near)
+    near_fine = pair_fine(near)
+    far_row = jnp.clip(far, 0, rows - 1)
+    far_columns = pair_columns(far_row)
+    far_fine = jnp.where(has_far, pair_fine(far_row), -(1 << 24))
+    to_mate.wait_recv()
+    mine, other = meta[...], close[4]
+    my_low = jnp.where(part == 0, mine, other)
+    my_high = jnp.where(part == 0, other, mine)
+    near_named = named_by(my_low, my_high, near_fine)
+    far_named = named_by(my_low, my_high, far_fine)
+    crowded = jnp.zeros((1, 1), jnp.int32)
+    for s in range(cap):
+        column = my_low[:, r_slots + s : r_slots + s + 1]
+        hits = (near_named & (near_columns == column)).astype(jnp.int32)
+        hits = hits + (far_named & (far_columns == column)).astype(jnp.int32)
+        held = jnp.sum(hits, axis=1, keepdims=True)
+        crowded = jnp.maximum(crowded, jnp.max(held, axis=0, keepdims=True))
+    over = jnp.maximum(near_total - 2 * list_slots, far_total - 2 * pass_slots)
+    over = jnp.maximum(over, crowded - JOBS)
+    over = (over > 0).astype(jnp.int32)
+    if groups > 2:
+        told[group] = jnp.broadcast_to(over, told.shape[1:])
+
+        def tell(ahead):
+            return remote(
+                told.at[group], told.at[group], told_sems.at[0], told_sems.at[1],
+                (row, lax.rem(group + ahead, groups)),
+            )
+
+        for ahead in range(1, groups):
+            tell(ahead).start()
+        wait_bytes(told.at[pl.ds(0, groups - 1)], told_sems.at[1])
+        over = told[0]
+        for other_group in range(1, groups):
+            over = over + told[other_group]
+
+    tile = pair_a.shape[1]
+    total_count = jnp.sum(own_counts, axis=0, keepdims=True)
+
+    def scan_copy(k, side):
+        other = row + (1 << k) if side == 0 else row - (1 << k)
+        return remote(
+            scan_out.at[k], scan_in.at[k, side], scan_sems.at[0, k, side], scan_sems.at[1, k, side],
+            (other, group),
+        )
+
+    scan_shape = scan_out.shape[1:]
+    scan_lane = lax.broadcasted_iota(jnp.int32, scan_shape, 1)
+    above_there = [row + (1 << k) < rows for k in range(rounds)]
+    below_there = [row - (1 << k) >= 0 for k in range(rounds)]
+
+    def scan_send(k, state):
+        scan_out[k] = state
+
+        @pl.when(above_there[k])
+        def _():
+            scan_copy(k, 0).start()
+
+        @pl.when(below_there[k])
+        def _():
+            scan_copy(k, 1).start()
+
+    def scan_take(k, state):
+        @pl.when(below_there[k])
+        def _():
+            scan_copy(k, 0).wait_recv()
+
+        @pl.when(above_there[k])
+        def _():
+            scan_copy(k, 1).wait_recv()
+
+        below = jnp.where((scan_lane < 2) & below_there[k], scan_in[k, 0], 0)
+        beyond = jnp.where((scan_lane == 2) & above_there[k], scan_in[k, 1], 0)
+        return state + below + beyond
+
+    state = jnp.where(
+        scan_lane == 0, jnp.broadcast_to(total_count, scan_shape),
+        jnp.where(scan_lane < 3, over, 0),
+    )
+    scan_send(0, state)
+    scans = 0
+
+    def scan_step():
+        nonlocal state, scans
+        state = scan_take(scans, state)
+        scans += 1
+        if scans < rounds:
+            scan_send(scans, state)
+
     mate_a.wait_recv()
     pick_copy.wait()
 
@@ -674,11 +767,6 @@
                 far_copy(index).wait_recv()
                 mate_copy(far_view(index), far_pair_sems).start()
 
-    near_columns = pair_columns(near)
-    near_fine = pair_fine(near)
-    far_row = jnp.clip(far, 0, rows - 1)
-    far_columns = pair_columns(far_row)
-    far_fine = jnp.where(has_far, pair_fine(far_row), -(1 << 24))
     early_copy.wait_recv()
 
     @pl.when(has_onward)
@@ -686,10 +774,8 @@
         early_far.start()
 
     mate_copy(early_view, near_pair_sems).start()
-    to_mate.wait_recv()
-    mine, other = meta[...], close[4]
-    my_low = jnp.where(part == 0, mine, other)
-    my_high = jnp.where(part == 0, other, mine)
+    if scans < rounds:
+        scan_step()
     far_need = need_of(my_low, my_high, far_columns, far_fine) * late
     far_places = jnp.where(far_need > 0, before(far_need), -1)
     far_at = landing(far_places, pass_slots, far_base, far_slots)
@@ -729,7 +815,6 @@
     while step < both:
         rank = rank + jnp.where(table_j >= step, pltpu.roll(rank, step, 1), 0)
         step *= 2
-    crowded = jnp.max(jnp.max(rank, axis=1, keepdims=True), axis=0, keepdims=True)
     job = jnp.where(away, (code - REMOTE) * both + table_j, -1)
     rank = jnp.where(away, rank - 1 + (table_lanes // both) * JOBS, -1)
     short = jnp.full(above, -1, jnp.int32)
@@ -744,72 +829,11 @@
     code_copy = pltpu.make_async_copy(tables, codes, table_sems.at[1])
     code_copy.start()
 
-    over = jnp.maximum(near_total - 2 * list_slots, far_total - 2 * pass_slots)
-    over = jnp.maximum(over, crowded - JOBS)
-    over = (over > 0).astype(jnp.int32)
-    told[group] = jnp.broadcast_to(over, told.shape[1:])
-
-    def tell(ahead):
-        return remote(
-            told.at[group], told.at[group], told_sems.at[0], told_sems.at[1],
-            (row, lax.rem(group + ahead, groups)),
-        )
-
-    for ahead in range(1, groups):
-        tell(ahead).start()
-
-    tile = pair_a.shape[1]
-    total_count = jnp.sum(own_counts, axis=0, keepdims=True)
-
-    def scan_copy(k, side):
-        other = row + (1 << k) if side == 0 else row - (1 << k)
-        return remote(
-            scan_out.at[k], scan_in.at[k, side], scan_sems.at[0, k, side], scan_sems.at[1, k, side],
-            (other, group),
-        )
-
-    scan_shape = scan_out.shape[1:]
-    scan_lane = lax.broadcasted_iota(jnp.int32, scan_shape, 1)
-    above_there = [row + (1 << k) < rows for k in range(rounds)]
-    below_there = [row - (1 << k) >= 0 for k in range(rounds)]
-
-    def scan_send(k, state):
-        scan_out[k] = state
-
-        @pl.when(above_there[k])
-        def _():
-            scan_copy(k, 0).start()
-
-        @pl.when(below_there[k])
-        def _():
-            scan_copy(k, 1).start()
-
-    def scan_take(k, state):
-        @pl.when(below_there[k])
-        def _():
-            scan_copy(k, 0).wait_recv()
-
-        @pl.when(above_there[k])
-        def _():
-            scan_copy(k, 1).wait_recv()
-
-        below = jnp.where((scan_lane < 2) & below_there[k], scan_in[k, 0], 0)
-        beyond = jnp.where((scan_lane == 2) & above_there[k], scan_in[k, 1], 0)
-        return state + below + beyond
-
-    wait_bytes(told.at[pl.ds(0, groups - 1)], told_sems.at[1])
-    over = told[0]
-    for other_group in range(1, groups):
-        over = over + told[other_group]
-    state = jnp.where(
-        scan_lane == 0, jnp.broadcast_to(total_count, scan_shape),
-        jnp.where(scan_lane < 3, over, 0),
-    )
-    scan_send(order[0], state)
-
     code_copy.wait()
     own_r.wait()
     mate_r.wait_recv()
+    if scans < rounds:
+        scan_step()
 
     def own_stage(c, carry):
         for index in range(0, half_cap, 2):
@@ -834,7 +858,6 @@
         return carry
 
     lag = 3
-    scans = 0
     for index in range(near_chunks):
         near_copy(index).wait_recv()
         if index < far_chunks:
@@ -847,17 +870,12 @@
         lax.fori_loop(
             index * row_count // near_chunks, (index + 1) * row_count // near_chunks, own_stage, 0
         )
-        if index > 0 and scans < rounds - 1:
-            state = scan_take(order[scans], state)
-            scans += 1
-            scan_send(order[scans], state)
+        if index % 3 == 1 and scans < rounds:
+            scan_step()
     for index in range(max(near_chunks - lag, -1), far_chunks):
         take_far(index)
     while scans < rounds:
-        state = scan_take(order[scans], state)
-        scans += 1
-        if scans < rounds:
-            scan_send(order[scans], state)
+        scan_step()
 
     flags = jnp.where((scan_lane == 1) | (scan_lane == 2), state, 0)
     flags = jnp.max(jnp.max(flags, axis=1, keepdims=True), axis=0, keepdims=True)
@@ -889,7 +907,7 @@
             out_ref[place] = total.astype(out_ref.dtype)
         return carry
 
-    lax.fori_loop(0, row_count, near_stage, 0)
+    lax.fori_loop(0, row_count, near_stage, 0, unroll=4)
 
     wait_bytes(close.at[pl.ds(0, 2)], close_sems.at[0, 0])
     to_mate.wait_send()
@@ -898,7 +916,8 @@
     early_copy.wait_send()
     place_copy.wait_send()
     wait_bytes(packed, near_send.at[0])
-    wait_bytes(told.at[pl.ds(0, groups - 1)], told_sems.at[0])
+    if groups > 2:
+        wait_bytes(told.at[pl.ds(0, groups - 1)], told_sems.at[0])
     wait_bytes(landed.at[pl.ds(0, near_slots)], near_pair_sems.at[0])
 
     @pl.when(has_onward)

time: 37.9 us -> 36.4 us (0.960)
  Pallas kernels: 34.6 us -> 32.9 us
    pallas_call x1, Pallas kernels: 34.6 us -> 32.9 us  [fused_body(): pl.pallas_call(functools.partial(fused_kernel, dims), out_shape=(jax.Shap...]
where the time goes in v3:
time: 36.4 us; the launch traced here: 35.9 us
  Pallas kernels  32.9 us (90%)
  local copies, waits for them, and re-layouts  1.5 us (4%)
  between operations  1.4 us (4%)
    pallas_call x1, Pallas kernels, fused_body(): pl.pallas_call(functools.partial(fused_kernel, dims), out_shape=(jax.Shap...  32.9 us
    unnamed x12, local copies, waits for them, and re-layouts  1.5 us

profile of v3, /device:TPU:0, one launch (start us, length us, event | category | flops | bytes accessed | tf_op | source)
XLA Modules:
  0.0 35.9 jit_solution(1721504070063288397)
XLA Ops:
  0.6 0.0 copy-start.4
  0.6 0.0 copy-start.3
  0.7 0.0 copy-start.2
  0.7 0.0 copy-start
  0.7 0.0 copy-start.1
  0.7 32.9 %fused.1 = (bf16[32,128,128]{2,1,0:T(8,128)(2,1)S(1)}, s32[1,8]{1,0:T(1,128)S(1)}, s32[1,1]{1,0:T(1,128)}) custom-call(s32[8,8]{1,0:T(8,128)} %r_cols_hbm.1, s32[8,8]{1,0:T(8,128)} %c_cols_hbm.1, s32[1,8]{1,0:T(1,128)} %bitcast.74, s32[7,256]{1,0:T(8,128)} %bitcast.73, bf16[56,128,128]{2,1,0:T(8,128)(2,1)} %bitcast.33, bf16[64,128,128]{2,1,0:T(8,128)(2,1)} %bitcast.69), custom_call_target="tpu_custom_call" | custom-call | tf_op jit(solution)/shard_map/fused/pallas_call | solution.py:994
  34.3 0.0 copy-done.4
  34.3 0.0 copy-done.3
  34.3 0.0 copy-done.2
  34.3 0.0 copy-done
  34.4 0.0 copy-done.1
  34.4 1.0 %copy.33 = bf16[8,4,128,128]{3,2,1,0:T(8,128)(2,1)} copy(bf16[8,4,128,128]{3,2,1,0:T(8,128)(2,1)S(1)} %get-tuple-element.183) | data formatting | bytes 2097152
  35.3 0.5 %copy.34 = s32[8]{0:T(128)} copy(s32[8]{0:T(128)S(1)} %get-tuple-element.184) | data formatting | bytes 64
  (1 shorter events, 0.0 us)
Async XLA Ops:
  0.6 33.7 %copy-start.4 = (s32[8]{0:T(128)S(1)}, s32[8]{0:T(128)}, u32[]{:S(2)}) copy-start(s32[8]{0:T(128)} %param.30) | copy-start | bytes 100
  0.6 33.7 %copy-start.3 = (s32[8,8]{1,0:T(8,128)S(1)}, s32[8,8]{1,0:T(8,128)}, u32[]{:S(2)}) copy-start(s32[8,8]{1,0:T(8,128)} %c_cols_hbm.1) | copy-start | bytes 772
  0.7 33.7 %copy-start.2 = (s32[256,7]{0,1:T(8,128)S(1)}, s32[256,7]{0,1:T(8,128)}, u32[]{:S(2)}) copy-start(s32[256,7]{0,1:T(8,128)} %param.28) | copy-start | bytes 21508
  0.7 33.7 %copy-start = (bf16[8,7,128,128]{3,2,1,0:T(8,128)(2,1)S(1)}, bf16[8,7,128,128]{3,2,1,0:T(8,128)(2,1)}, u32[]{:S(2)}) copy-start(bf16[8,7,128,128]{3,2,1,0:T(8,128)(2,1)} %param.27) | copy-start | bytes 5505028
  0.7 33.7 %copy-start.1 = (s32[8,8]{1,0:T(8,128)S(1)}, s32[8,8]{1,0:T(8,128)}, u32[]{:S(2)}) copy-start(s32[8,8]{1,0:T(8,128)} %r_cols_hbm.1) | copy-start | bytes 772

commit v4 on v3

--- a/solution.py
+++ b/solution.py
@@ -402,23 +402,23 @@
     c_tiles = c_tiles.astype(jnp.bfloat16)
     return (c_tiles.reshape(row_count, own_cap, tile, tile), plan[2, :row_count])
 
-LIST_SLOTS = 27
 PASS_SLOTS = 15
 CHUNK = 3
+LAST_CHUNKS = (3, 3, 3, 2)
 JOBS = 4
 REMOTE = 1 << 14
 
 
 def fused_kernel(
     dims, r_cols_hbm, c_cols_hbm, counts_hbm, columns_hbm, a_ref, r_ref,
-    out_ref, offsets_ref, flag_ref,
-    r_cols_ref, c_cols_ref, counts_ref, columns_ref,
+    out_ref, offsets_ref, flag_hbm,
+    flag_ref, r_cols_ref, c_cols_ref, counts_ref, columns_ref,
     meta, close, placing, pair_a, pair_r, packed, landed, sums, tables, codes, picks,
     told, scan_out, scan_in,
     local_sems, close_sems, pair_sems, place_sems, early_sems, near_sems, near_send,
     near_pair_sems, far_sems, far_send, far_pair_sems, table_sems, told_sems, scan_sems,
 ):
-    (rows, groups, local_rows, op_slots, r_slots, cap, width, list_slots, pass_slots, chunk) = dims
+    (rows, groups, local_rows, op_slots, r_slots, cap, width, list_slots, pass_slots, chunks) = dims
     pairs = groups // 2
     tiles = local_rows * op_slots
     span = 2 * local_rows
@@ -430,8 +430,8 @@
     early = op_slots
     near_slots = early + list_slots
     far_slots = early + pass_slots
-    near_chunks = list_slots // chunk
-    far_chunks = pass_slots // chunk
+    near_chunks = len(chunks)
+    far_chunks = sum(start < pass_slots for start, _ in chunks)
     far_base = 2 * near_slots
     zero_near = 2 * (near_slots + far_slots)
     zero_own = 2 * tiles
@@ -723,17 +723,19 @@
     pick_copy.wait()
 
     def near_view(index):
-        return landed.at[pl.ds(part * near_slots + early + index * chunk, chunk)]
+        start, size = chunks[index]
+        return landed.at[pl.ds(part * near_slots + early + start, size)]
 
     def near_copy(index):
         return remote(
-            packed.at[pl.ds(index * chunk, chunk)], near_view(index),
+            packed.at[pl.ds(*chunks[index])], near_view(index),
             near_send.at[0], near_sems.at[index], (near, group),
         )
 
     def pack(index):
-        for extra in range(chunk):
-            packed[index * chunk + extra] = pair_a[picks[0, index * chunk + extra]]
+        start, size = chunks[index]
+        for slot in range(start, start + size):
+            packed[slot] = pair_a[picks[0, slot]]
 
     pack(0)
     for index in range(near_chunks):
@@ -748,7 +750,8 @@
     early_far_view = landed.at[pl.ds(far_base + part * far_slots, early)]
 
     def far_view(index):
-        return landed.at[pl.ds(far_base + part * far_slots + early + index * chunk, chunk)]
+        start, size = chunks[index]
+        return landed.at[pl.ds(far_base + part * far_slots + early + start, size)]
 
     early_far = remote(early_view, early_far_view, far_send.at[0], far_sems.at[far_chunks], (onward, group))
 
@@ -879,7 +882,9 @@
 
     flags = jnp.where((scan_lane == 1) | (scan_lane == 2), state, 0)
     flags = jnp.max(jnp.max(flags, axis=1, keepdims=True), axis=0, keepdims=True)
-    flag_ref[...] = (flags > 0).astype(jnp.int32)
+    flag_ref[...] = jnp.broadcast_to((flags > 0).astype(jnp.int32), flag_ref.shape)
+    flag_copy = pltpu.make_async_copy(flag_ref, flag_hbm, table_sems.at[0])
+    flag_copy.start()
     reached = jnp.where(scan_lane == 0, state, 0)
     reached = jnp.max(jnp.max(reached, axis=1, keepdims=True), axis=0, keepdims=True)
     earlier = lax.broadcasted_iota(jnp.int32, small, 0) < lax.broadcasted_iota(jnp.int32, small, 1)
@@ -909,6 +914,7 @@
 
     lax.fori_loop(0, row_count, near_stage, 0, unroll=4)
 
+    flag_copy.wait()
     wait_bytes(close.at[pl.ds(0, 2)], close_sems.at[0, 0])
     to_mate.wait_send()
     mate_a.wait_send()
@@ -937,6 +943,17 @@
         @pl.when(below_there[k])
         def _():
             scan_copy(k, 1).wait_send()
+
+
+def put_kernel(tiles_ref, offsets_ref, tiles_out, offsets_out, sems):
+    copies = [
+        pltpu.make_async_copy(tiles_ref, tiles_out, sems.at[0]),
+        pltpu.make_async_copy(offsets_ref, offsets_out, sems.at[1]),
+    ]
+    for copy in copies:
+        copy.start()
+    for copy in copies:
+        copy.wait()
 
 
 def pair_sum_kernel(pairs, own, part_ref, landed, send_sems, recv_sems):
@@ -976,11 +993,16 @@
     own_cap = cap // groups
     half_cap = cap // 2
     width = -(-2 * tiles // 128) * 128
-    list_slots = min(LIST_SLOTS, -(-tiles // CHUNK) * CHUNK)
-    pass_slots = min(PASS_SLOTS, list_slots)
-    dims = (rows, groups, local_rows, op_slots, r_slots, cap, width, list_slots, pass_slots, CHUNK)
-    near_chunks = list_slots // CHUNK
-    far_chunks = pass_slots // CHUNK
+    chunks = []
+    for size in [CHUNK] * (PASS_SLOTS // CHUNK) + list(LAST_CHUNKS):
+        chunks.append((sum(before for _, before in chunks), size))
+    list_slots = sum(size for _, size in chunks)
+    pass_slots = PASS_SLOTS
+    dims = (
+        rows, groups, local_rows, op_slots, r_slots, cap, width, list_slots, pass_slots, tuple(chunks)
+    )
+    near_chunks = len(chunks)
+    far_chunks = PASS_SLOTS // CHUNK
     near_slots = op_slots + list_slots
     far_slots = op_slots + pass_slots
     rounds = (rows - 1).bit_length()
@@ -996,11 +1018,12 @@
         out_shape=(
             jax.ShapeDtypeStruct((pairs * own, tile, tile), out_dtype),
             jax.ShapeDtypeStruct((1, row_count), jnp.int32),
-            jax.ShapeDtypeStruct((1, 1), jnp.int32),
+            jax.ShapeDtypeStruct((1, 128), jnp.int32),
         ),
         in_specs=[anywhere] * 6,
-        out_specs=(vmem, vmem, vmem),
+        out_specs=(vmem, vmem, anywhere),
         scratch_shapes=[
+            pltpu.VMEM((1, 128), jnp.int32),
             pltpu.VMEM(r_cols.shape, jnp.int32),
             pltpu.VMEM(c_cols.shape, jnp.int32),
             pltpu.VMEM((1, row_count), jnp.int32),
@@ -1074,7 +1097,21 @@
     def keep(c_tiles, offsets, *args):
         return c_tiles, offsets
 
-    return lax.cond(flag > 0, again, keep, c_tiles, offsets, *args)
+    c_tiles, offsets = lax.cond(flag > 0, again, keep, c_tiles, offsets, *args)
+    vmem = pl.BlockSpec(memory_space=pltpu.VMEM)
+    anywhere = pl.BlockSpec(memory_space=pl.ANY)
+    c_tiles, offsets = pl.pallas_call(
+        put_kernel,
+        out_shape=(
+            jax.ShapeDtypeStruct(c_tiles.shape, c_tiles.dtype),
+            jax.ShapeDtypeStruct((1,) + offsets.shape, offsets.dtype),
+        ),
+        in_specs=[vmem, vmem],
+        out_specs=(anywhere, anywhere),
+        scratch_shapes=[pltpu.SemaphoreType.DMA((2,))],
+        name="put",
+    )(c_tiles, offsets[None, :])
+    return c_tiles, offsets[0]
 
 
 def solution(mesh):

time: 36.4 us -> 34.6 us (0.951)
  local copies, waits for them, and re-layouts: 1.5 us -> 0.02 us
    unnamed x12 -> x10, local copies, waits for them, and re-layouts: 1.5 us -> 0.02 us
    pallas_call x1, Pallas kernels: 32.9 us -> 31.7 us  [fused_body(): pl.pallas_call(functools.partial(fused_kernel, dims), out_shape=(jax.Shap...]
    pallas_call x0 -> x1, Pallas kernels: none -> 0.99 us  [body(): pl.pallas_call(put_kernel, out_shape=(jax.ShapeDtypeStruct(c_tiles.shape,...]
where the time goes in v4:
time: 34.6 us; the launch traced here: 34.1 us
  Pallas kernels  32.7 us (95%)
  between operations  1.41 us (4%)
    pallas_call x1, Pallas kernels, fused_body(): pl.pallas_call(functools.partial(fused_kernel, dims), out_shape=(jax.Shap...  31.7 us
    pallas_call x1, Pallas kernels, body(): pl.pallas_call(put_kernel, out_shape=(jax.ShapeDtypeStruct(c_tiles.shape,...  0.99 us

profile of v4, /device:TPU:0, one launch (start us, length us, event | category | flops | bytes accessed | tf_op | source)
XLA Modules:
  0.0 34.1 jit_solution(3801731269510153396)
XLA Ops:
  0.6 0.0 copy-start.4
  0.6 0.0 copy-start.3
  0.7 0.0 copy-start.2
  0.7 0.0 copy-start
  0.7 0.0 copy-start.1
  0.7 31.7 %fused.1 = (bf16[32,128,128]{2,1,0:T(8,128)(2,1)S(1)}, s32[1,8]{1,0:T(1,128)S(1)}, s32[1,128]{1,0:T(1,128)}) custom-call(s32[8,8]{1,0:T(8,128)} %r_cols_hbm.1, s32[8,8]{1,0:T(8,128)} %c_cols_hbm.1, s32[1,8]{1,0:T(1,128)} %bitcast.71, s32[7,256]{1,0:T(8,128)} %bitcast.70, bf16[56,128,128]{2,1,0:T(8,128)(2,1)} %bitcast.31, bf16[64,128,128]{2,1,0:T(8,128)(2,1)} %bitcast.67), custom_call_target="tpu_custom_call" | custom-call | tf_op jit(solution)/shard_map/fused/pallas_call | solution.py:1016
  33.0 0.0 copy-done.4
  33.1 0.0 copy-done.3
  33.1 0.0 copy-done.2
  33.1 0.0 copy-done
  33.1 0.0 copy-done.1
  33.1 1.0 %put.1 = (bf16[8,4,128,128]{3,2,1,0:T(8,128)(2,1)}, s32[1,8]{1,0:T(1,128)}) custom-call(bf16[8,4,128,128]{3,2,1,0:T(8,128)(2,1)S(1)} %bitcast.69, s32[1,8]{1,0:T(1,128)S(1)} %get-tuple-element.183.offsets_ref), custom_call_target="tpu_custom_call" | custom-call | tf_op jit(solution)/shard_map/put/pallas_call | solution.py:1103
  (1 shorter events, 0.0 us)
Async XLA Ops:
  0.6 32.4 %copy-start.4 = (s32[8]{0:T(128)S(1)}, s32[8]{0:T(128)}, u32[]{:S(2)}) copy-start(s32[8]{0:T(128)} %param.30) | copy-start | bytes 100
  0.6 32.4 %copy-start.3 = (s32[8,8]{1,0:T(8,128)S(1)}, s32[8,8]{1,0:T(8,128)}, u32[]{:S(2)}) copy-start(s32[8,8]{1,0:T(8,128)} %c_cols_hbm.1) | copy-start | bytes 772
  0.7 32.4 %copy-start.2 = (s32[256,7]{0,1:T(8,128)S(1)}, s32[256,7]{0,1:T(8,128)}, u32[]{:S(2)}) copy-start(s32[256,7]{0,1:T(8,128)} %param.28) | copy-start | bytes 21508
  0.7 32.4 %copy-start = (bf16[8,7,128,128]{3,2,1,0:T(8,128)(2,1)S(1)}, bf16[8,7,128,128]{3,2,1,0:T(8,128)(2,1)}, u32[]{:S(2)}) copy-start(bf16[8,7,128,128]{3,2,1,0:T(8,128)(2,1)} %param.27) | copy-start | bytes 5505028
  0.7 32.4 %copy-start.1 = (s32[8,8]{1,0:T(8,128)S(1)}, s32[8,8]{1,0:T(8,128)}, u32[]{:S(2)}) copy-start(s32[8,8]{1,0:T(8,128)} %r_cols_hbm.1) | copy-start | bytes 772

commit v5 on v4

--- a/solution.py
+++ b/solution.py
@@ -402,6 +402,7 @@
     c_tiles = c_tiles.astype(jnp.bfloat16)
     return (c_tiles.reshape(row_count, own_cap, tile, tile), plan[2, :row_count])
 
+EARLY = 7
 PASS_SLOTS = 15
 CHUNK = 3
 LAST_CHUNKS = (3, 3, 3, 2)
@@ -427,11 +428,12 @@
     both = 2 * r_slots
     row_count = r_cols_ref.shape[0]
     live = r_slots + cap
-    early = op_slots
+    early = min(EARLY, op_slots)
     near_slots = early + list_slots
     far_slots = early + pass_slots
     near_chunks = len(chunks)
     far_chunks = sum(start < pass_slots for start, _ in chunks)
+    last_slots = chunks[-1][1]
     far_base = 2 * near_slots
     zero_near = 2 * (near_slots + far_slots)
     zero_own = 2 * tiles
@@ -543,7 +545,7 @@
     lane_core = lax.rem(lanes, span) // local_rows
     lane_local = lax.rem(lanes, local_rows)
     lane_tile = lane_core * tiles + lane_local * op_slots + lane_slot
-    late = jnp.where(lane_local > 0, 1, 0)
+    late = jnp.where((lane_local > 0) | (lane_slot >= early), 1, 0)
 
     def pair_columns(which_row):
         start = (which_row * groups + first_group) * local_rows
@@ -569,12 +571,20 @@
             named = named | (fine == meta_high[:, j : j + 1])
         return named
 
+    def need_by_core(meta_low, meta_high, columns, fine):
+        named = named_by(meta_low, meta_high, fine)
+        needs = []
+        for core in range(2):
+            wanted = jnp.zeros(named.shape, jnp.bool_)
+            for s in range(cap):
+                if s // own_cap % 2 == core:
+                    wanted = wanted | (columns == meta_low[:, r_slots + s : r_slots + s + 1])
+            needs.append(jnp.max((named & wanted).astype(jnp.int32), axis=0, keepdims=True))
+        return needs
+
     def need_of(meta_low, meta_high, columns, fine):
-        named = named_by(meta_low, meta_high, fine)
-        wanted = columns == meta_low[:, r_slots : r_slots + 1]
-        for s in range(1, cap):
-            wanted = wanted | (columns == meta_low[:, r_slots + s : r_slots + s + 1])
-        return jnp.max((named & wanted).astype(jnp.int32), axis=0, keepdims=True)
+        low, high = need_by_core(meta_low, meta_high, columns, fine)
+        return jnp.maximum(low, high)
 
     def before(need):
         total = need
@@ -593,42 +603,6 @@
     own_columns = pair_columns(row)
     own_fine = pair_fine(row)
 
-    @pl.when(has_far)
-    def _():
-        wait_bytes(close.at[pl.ds(2, 2)], close_sems.at[1, 1])
-
-    @pl.when(jnp.logical_not(has_far))
-    def _():
-        close[2] = jnp.full(close.shape[1:], -9, jnp.int32)
-        close[3] = jnp.full(close.shape[1:], -9, jnp.int32)
-
-    need_far = need_of(close[2], close[3], own_columns, own_fine) * late
-    far_before = before(need_far)
-    far_total = jnp.sum(need_far, axis=1, keepdims=True)
-    wait_bytes(close.at[pl.ds(0, 2)], close_sems.at[1, 0])
-    need_near = need_of(close[0], close[1], own_columns, own_fine) * late
-    need_only = need_near * (1 - need_far)
-    near_total = far_total + jnp.sum(need_only, axis=1, keepdims=True)
-    places = jnp.where(
-        need_far > 0, far_before, jnp.where(need_only > 0, before(need_only) + far_total, -1)
-    )
-    pick_rows = -(-list_slots // 8) * 8
-    slot_down = lax.broadcasted_iota(jnp.int32, (pick_rows, width), 0)
-    chosen = jnp.broadcast_to(places, (pick_rows, width)) == 2 * slot_down + part
-    picked = jnp.sum(
-        jnp.where(chosen, jnp.broadcast_to(lane_tile, (pick_rows, width)), 0), axis=1, keepdims=True
-    )
-    across = lax.broadcasted_iota(jnp.int32, (pick_rows, width), 1)
-    pick_row = jnp.sum(
-        jnp.where(slot_down == across, jnp.broadcast_to(picked, (pick_rows, width)), 0),
-        axis=0, keepdims=True,
-    )
-    tables[0:8, :] = jnp.broadcast_to(pick_row, (8, width))
-    pick_copy = pltpu.make_async_copy(tables.at[pl.ds(0, 8)], picks, table_sems.at[0])
-    pick_copy.start()
-    placing[0] = jnp.broadcast_to(landing(places, list_slots, 0, near_slots), placing.shape[1:])
-    place_copy = remote(placing.at[0], placing.at[1], place_sems.at[0], place_sems.at[1], (near, group))
-    place_copy.start()
     near_columns = pair_columns(near)
     near_fine = pair_fine(near)
     far_row = jnp.clip(far, 0, rows - 1)
@@ -647,7 +621,57 @@
         hits = hits + (far_named & (far_columns == column)).astype(jnp.int32)
         held = jnp.sum(hits, axis=1, keepdims=True)
         crowded = jnp.maximum(crowded, jnp.max(held, axis=0, keepdims=True))
-    over = jnp.maximum(near_total - 2 * list_slots, far_total - 2 * pass_slots)
+
+    wait_bytes(close.at[pl.ds(0, 2)], close_sems.at[1, 0])
+    near_low, near_high = [
+        need * late for need in need_by_core(close[0], close[1], own_columns, own_fine)
+    ]
+
+    @pl.when(has_far)
+    def _():
+        wait_bytes(close.at[pl.ds(2, 2)], close_sems.at[1, 1])
+
+    @pl.when(jnp.logical_not(has_far))
+    def _():
+        close[2] = jnp.full(close.shape[1:], -9, jnp.int32)
+        close[3] = jnp.full(close.shape[1:], -9, jnp.int32)
+
+    need_far = need_of(close[2], close[3], own_columns, own_fine) * late
+    need_only = jnp.maximum(near_low, near_high) * (1 - need_far)
+    lone_low = need_only * (1 - near_high)
+    lone_high = need_only * (1 - near_low)
+    counts_before = before(jnp.concatenate([need_far, lone_low, lone_high], axis=0))
+    far_before, low_before, high_before = [counts_before[x : x + 1] for x in range(3)]
+    far_total = jnp.sum(need_far, axis=1, keepdims=True)
+    last_low = (lone_low > 0) & (low_before < last_slots)
+    last_high = (lone_high > 0) & (high_before < last_slots)
+    need_rest = jnp.where(last_low | last_high, 0, need_only)
+    near_total = far_total + jnp.sum(need_rest, axis=1, keepdims=True)
+    places = jnp.where(
+        need_far > 0, far_before, jnp.where(need_rest > 0, before(need_rest) + far_total, -1)
+    )
+    last_first = list_slots - last_slots
+    places = jnp.where(places < 2 * last_first, places, -1)
+    places = jnp.where(last_low, 2 * (last_first + low_before), places)
+    places = jnp.where(last_high, 2 * (last_first + high_before) + 1, places)
+    pick_rows = -(-list_slots // 8) * 8
+    slot_down = lax.broadcasted_iota(jnp.int32, (pick_rows, width), 0)
+    chosen = jnp.broadcast_to(places, (pick_rows, width)) == 2 * slot_down + part
+    picked = jnp.sum(
+        jnp.where(chosen, jnp.broadcast_to(lane_tile, (pick_rows, width)), 0), axis=1, keepdims=True
+    )
+    across = lax.broadcasted_iota(jnp.int32, (pick_rows, width), 1)
+    pick_row = jnp.sum(
+        jnp.where(slot_down == across, jnp.broadcast_to(picked, (pick_rows, width)), 0),
+        axis=0, keepdims=True,
+    )
+    tables[0:8, :] = jnp.broadcast_to(pick_row, (8, width))
+    pick_copy = pltpu.make_async_copy(tables.at[pl.ds(0, 8)], picks, table_sems.at[0])
+    pick_copy.start()
+    placing[0] = jnp.broadcast_to(landing(places, list_slots, 0, near_slots), placing.shape[1:])
+    place_copy = remote(placing.at[0], placing.at[1], place_sems.at[0], place_sems.at[1], (near, group))
+    place_copy.start()
+    over = jnp.maximum(near_total - 2 * (list_slots - last_slots), far_total - 2 * pass_slots)
     over = jnp.maximum(over, crowded - JOBS)
     over = (over > 0).astype(jnp.int32)
     if groups > 2:
@@ -867,7 +891,8 @@
             @pl.when(has_onward)
             def _():
                 far_copy(index).start()
-        mate_copy(near_view(index), near_pair_sems).start()
+        if index + 1 < near_chunks:
+            mate_copy(near_view(index), near_pair_sems).start()
         if -1 <= index - lag < far_chunks:
             take_far(index - lag)
         lax.fori_loop(
@@ -892,7 +917,7 @@
     inner_sum = jnp.sum(jnp.where(earlier, counts, 0), axis=0, keepdims=True)
     offsets_ref[...] = inner_sum + (reached - total_count)
 
-    wait_bytes(landed.at[pl.ds(0, near_slots)], near_pair_sems.at[1])
+    wait_bytes(landed.at[pl.ds(0, near_slots - last_slots)], near_pair_sems.at[1])
 
     @pl.when(has_far)
     def _():
@@ -924,7 +949,7 @@
     wait_bytes(packed, near_send.at[0])
     if groups > 2:
         wait_bytes(told.at[pl.ds(0, groups - 1)], told_sems.at[0])
-    wait_bytes(landed.at[pl.ds(0, near_slots)], near_pair_sems.at[0])
+    wait_bytes(landed.at[pl.ds(0, near_slots - last_slots)], near_pair_sems.at[0])
 
     @pl.when(has_onward)
     def _():
@@ -1003,8 +1028,9 @@
     )
     near_chunks = len(chunks)
     far_chunks = PASS_SLOTS // CHUNK
-    near_slots = op_slots + list_slots
-    far_slots = op_slots + pass_slots
+    early = min(EARLY, op_slots)
+    near_slots = early + list_slots
+    far_slots = early + pass_slots
     rounds = (rows - 1).bit_length()
     dtype = a_tiles.dtype
     out_dtype = jnp.bfloat16 if pairs == 1 else jnp.float32

time: 34.6 us -> 34.3 us (level)
  no operation moved by 1% of the time
where the time goes in v5:
time: 34.3 us; the launch traced here: 34.1 us
  Pallas kernels  32.7 us (95%)
  between operations  1.41 us (4%)
    pallas_call x1, Pallas kernels, fused_body(): pl.pallas_call(functools.partial(fused_kernel, dims), out_shape=(jax.Shap...  31.7 us
    pallas_call x1, Pallas kernels, body(): pl.pallas_call(put_kernel, out_shape=(jax.ShapeDtypeStruct(c_tiles.shape,...  0.99 us

profile of v5, /device:TPU:0, one launch (start us, length us, event | category | flops | bytes accessed | tf_op | source)
XLA Modules:
  0.0 34.1 jit_solution(2885375505905797654)
XLA Ops:
  0.6 0.0 copy-start.4
  0.6 0.0 copy-start.3
  0.7 0.0 copy-start.2
  0.7 0.0 copy-start
  0.7 0.0 copy-start.1
  0.7 31.7 %fused.1 = (bf16[32,128,128]{2,1,0:T(8,128)(2,1)S(1)}, s32[1,8]{1,0:T(1,128)S(1)}, s32[1,128]{1,0:T(1,128)}) custom-call(s32[8,8]{1,0:T(8,128)} %r_cols_hbm.1, s32[8,8]{1,0:T(8,128)} %c_cols_hbm.1, s32[1,8]{1,0:T(1,128)} %bitcast.71, s32[7,256]{1,0:T(8,128)} %bitcast.70, bf16[56,128,128]{2,1,0:T(8,128)(2,1)} %bitcast.31, bf16[64,128,128]{2,1,0:T(8,128)(2,1)} %bitcast.67), custom_call_target="tpu_custom_call" | custom-call | tf_op jit(solution)/shard_map/fused/pallas_call | solution.py:1042
  33.0 0.0 copy-done.4
  33.1 0.0 copy-done.3
  33.1 0.0 copy-done.2
  33.1 0.0 copy-done
  33.1 0.0 copy-done.1
  33.1 1.0 %put.1 = (bf16[8,4,128,128]{3,2,1,0:T(8,128)(2,1)}, s32[1,8]{1,0:T(1,128)}) custom-call(bf16[8,4,128,128]{3,2,1,0:T(8,128)(2,1)S(1)} %bitcast.69, s32[1,8]{1,0:T(1,128)S(1)} %get-tuple-element.183.offsets_ref), custom_call_target="tpu_custom_call" | custom-call | tf_op jit(solution)/shard_map/put/pallas_call | solution.py:1129
  (1 shorter events, 0.0 us)
Async XLA Ops:
  0.6 32.4 %copy-start.4 = (s32[8]{0:T(128)S(1)}, s32[8]{0:T(128)}, u32[]{:S(2)}) copy-start(s32[8]{0:T(128)} %param.30) | copy-start | bytes 100
  0.6 32.4 %copy-start.3 = (s32[8,8]{1,0:T(8,128)S(1)}, s32[8,8]{1,0:T(8,128)}, u32[]{:S(2)}) copy-start(s32[8,8]{1,0:T(8,128)} %c_cols_hbm.1) | copy-start | bytes 772
  0.7 32.4 %copy-start.2 = (s32[256,7]{0,1:T(8,128)S(1)}, s32[256,7]{0,1:T(8,128)}, u32[]{:S(2)}) copy-start(s32[256,7]{0,1:T(8,128)} %param.28) | copy-start | bytes 21508
  0.7 32.4 %copy-start = (bf16[8,7,128,128]{3,2,1,0:T(8,128)(2,1)S(1)}, bf16[8,7,128,128]{3,2,1,0:T(8,128)(2,1)}, u32[]{:S(2)}) copy-start(bf16[8,7,128,128]{3,2,1,0:T(8,128)(2,1)} %param.27) | copy-start | bytes 5505028
  0.7 32.4 %copy-start.1 = (s32[8,8]{1,0:T(8,128)S(1)}, s32[8,8]{1,0:T(8,128)}, u32[]{:S(2)}) copy-start(s32[8,8]{1,0:T(8,128)} %r_cols_hbm.1) | copy-start | bytes 772

commit v6 on v5

--- a/solution.py
+++ b/solution.py
@@ -640,15 +640,20 @@
     need_only = jnp.maximum(near_low, near_high) * (1 - need_far)
     lone_low = need_only * (1 - near_high)
     lone_high = need_only * (1 - near_low)
-    counts_before = before(jnp.concatenate([need_far, lone_low, lone_high], axis=0))
-    far_before, low_before, high_before = [counts_before[x : x + 1] for x in range(3)]
-    far_total = jnp.sum(need_far, axis=1, keepdims=True)
+    lists = jnp.concatenate([need_far, need_only, lone_low, lone_high], axis=0)
+    ahead_in = before(lists)
+    totals = jnp.sum(lists, axis=1, keepdims=True)
+    far_before, only_before, low_before, high_before = [ahead_in[x : x + 1] for x in range(4)]
+    far_total, only_total, low_total, high_total = [totals[x : x + 1] for x in range(4)]
     last_low = (lone_low > 0) & (low_before < last_slots)
     last_high = (lone_high > 0) & (high_before < last_slots)
     need_rest = jnp.where(last_low | last_high, 0, need_only)
-    near_total = far_total + jnp.sum(need_rest, axis=1, keepdims=True)
+    near_total = far_total + only_total
+    near_total = near_total - jnp.minimum(low_total, last_slots) - jnp.minimum(high_total, last_slots)
+    rest_before = only_before - jnp.minimum(low_before, last_slots)
+    rest_before = rest_before - jnp.minimum(high_before, last_slots)
     places = jnp.where(
-        need_far > 0, far_before, jnp.where(need_rest > 0, before(need_rest) + far_total, -1)
+        need_far > 0, far_before, jnp.where(need_rest > 0, rest_before + far_total, -1)
     )
     last_first = list_slots - last_slots
     places = jnp.where(places < 2 * last_first, places, -1)
@@ -884,23 +889,25 @@
             sums[c * half_cap + index + 1] = total[:, tile:]
         return carry
 
+    def share(index):
+        return min(index * row_count // (near_chunks - 1), row_count)
+
     lag = 3
-    for index in range(near_chunks):
+    for index in range(near_chunks - 1):
         near_copy(index).wait_recv()
         if index < far_chunks:
             @pl.when(has_onward)
             def _():
                 far_copy(index).start()
-        if index + 1 < near_chunks:
-            mate_copy(near_view(index), near_pair_sems).start()
+        mate_copy(near_view(index), near_pair_sems).start()
         if -1 <= index - lag < far_chunks:
             take_far(index - lag)
         lax.fori_loop(
-            index * row_count // near_chunks, (index + 1) * row_count // near_chunks, own_stage, 0
+            share(index), share(index + 1), own_stage, 0
         )
         if index % 3 == 1 and scans < rounds:
             scan_step()
-    for index in range(max(near_chunks - lag, -1), far_chunks):
+    for index in range(max(near_chunks - 1 - lag, -1), far_chunks):
         take_far(index)
     while scans < rounds:
         scan_step()
@@ -917,6 +924,7 @@
     inner_sum = jnp.sum(jnp.where(earlier, counts, 0), axis=0, keepdims=True)
     offsets_ref[...] = inner_sum + (reached - total_count)
 
+    near_copy(near_chunks - 1).wait_recv()
     wait_bytes(landed.at[pl.ds(0, near_slots - last_slots)], near_pair_sems.at[1])
 
     @pl.when(has_far)
@@ -937,7 +945,7 @@
             out_ref[place] = total.astype(out_ref.dtype)
         return carry
 
-    lax.fori_loop(0, row_count, near_stage, 0, unroll=4)
+    lax.fori_loop(0, row_count, near_stage, 0, unroll=8)
 
     flag_copy.wait()
     wait_bytes(close.at[pl.ds(0, 2)], close_sems.at[0, 0])

time: 34.3 us -> 33.6 us (0.980)
  Pallas kernels: 32.7 us -> 32.1 us
    pallas_call x1, Pallas kernels: 31.7 us -> 31.1 us  [fused_body(): pl.pallas_call(functools.partial(fused_kernel, dims), out_shape=(jax.Shap...]
where the time goes in v6:
time: 33.6 us; the launch traced here: 33.5 us
  Pallas kernels  32.1 us (96%)
  between operations  1.41 us (4%)
    pallas_call x1, Pallas kernels, fused_body(): pl.pallas_call(functools.partial(fused_kernel, dims), out_shape=(jax.Shap...  31.1 us
    pallas_call x1, Pallas kernels, body(): pl.pallas_call(put_kernel, out_shape=(jax.ShapeDtypeStruct(c_tiles.shape,...  0.99 us

profile of v6, /device:TPU:0, one launch (start us, length us, event | category | flops | bytes accessed | tf_op | source)
XLA Modules:
  0.0 33.5 jit_solution(2075104327228394894)
XLA Ops:
  0.6 0.0 copy-start.4
  0.6 0.0 copy-start.3
  0.7 0.0 copy-start.2
  0.7 0.0 copy-start
  0.7 0.0 copy-start.1
  0.7 31.1 %fused.1 = (bf16[32,128,128]{2,1,0:T(8,128)(2,1)S(1)}, s32[1,8]{1,0:T(1,128)S(1)}, s32[1,128]{1,0:T(1,128)}) custom-call(s32[8,8]{1,0:T(8,128)} %r_cols_hbm.1, s32[8,8]{1,0:T(8,128)} %c_cols_hbm.1, s32[1,8]{1,0:T(1,128)} %bitcast.71, s32[7,256]{1,0:T(8,128)} %bitcast.70, bf16[56,128,128]{2,1,0:T(8,128)(2,1)} %bitcast.31, bf16[64,128,128]{2,1,0:T(8,128)(2,1)} %bitcast.67), custom_call_target="tpu_custom_call" | custom-call | tf_op jit(solution)/shard_map/fused/pallas_call | solution.py:1050
  32.4 0.0 copy-done.4
  32.4 0.0 copy-done.3
  32.5 0.0 copy-done.2
  32.5 0.0 copy-done
  32.5 0.0 copy-done.1
  32.5 1.0 %put.1 = (bf16[8,4,128,128]{3,2,1,0:T(8,128)(2,1)}, s32[1,8]{1,0:T(1,128)}) custom-call(bf16[8,4,128,128]{3,2,1,0:T(8,128)(2,1)S(1)} %bitcast.69, s32[1,8]{1,0:T(1,128)S(1)} %get-tuple-element.183.offsets_ref), custom_call_target="tpu_custom_call" | custom-call | tf_op jit(solution)/shard_map/put/pallas_call | solution.py:1137
  (1 shorter events, 0.0 us)
Async XLA Ops:
  0.6 31.8 %copy-start.4 = (s32[8]{0:T(128)S(1)}, s32[8]{0:T(128)}, u32[]{:S(2)}) copy-start(s32[8]{0:T(128)} %param.30) | copy-start | bytes 100
  0.6 31.8 %copy-start.3 = (s32[8,8]{1,0:T(8,128)S(1)}, s32[8,8]{1,0:T(8,128)}, u32[]{:S(2)}) copy-start(s32[8,8]{1,0:T(8,128)} %c_cols_hbm.1) | copy-start | bytes 772
  0.7 31.8 %copy-start.2 = (s32[256,7]{0,1:T(8,128)S(1)}, s32[256,7]{0,1:T(8,128)}, u32[]{:S(2)}) copy-start(s32[256,7]{0,1:T(8,128)} %param.28) | copy-start | bytes 21508
  0.7 31.8 %copy-start = (bf16[8,7,128,128]{3,2,1,0:T(8,128)(2,1)S(1)}, bf16[8,7,128,128]{3,2,1,0:T(8,128)(2,1)}, u32[]{:S(2)}) copy-start(bf16[8,7,128,128]{3,2,1,0:T(8,128)(2,1)} %param.27) | copy-start | bytes 5505028
  0.7 31.8 %copy-start.1 = (s32[8,8]{1,0:T(8,128)S(1)}, s32[8,8]{1,0:T(8,128)}, u32[]{:S(2)}) copy-start(s32[8,8]{1,0:T(8,128)} %r_cols_hbm.1) | copy-start | bytes 772

commit v7 on v6

--- a/solution.py
+++ b/solution.py
@@ -403,6 +403,7 @@
     return (c_tiles.reshape(row_count, own_cap, tile, tile), plan[2, :row_count])
 
 EARLY = 7
+SCAN_AT = (1, 2, 5)
 PASS_SLOTS = 15
 CHUNK = 3
 LAST_CHUNKS = (3, 3, 3, 2)
@@ -864,8 +865,6 @@
     code_copy.wait()
     own_r.wait()
     mate_r.wait_recv()
-    if scans < rounds:
-        scan_step()
 
     def own_stage(c, carry):
         for index in range(0, half_cap, 2):
@@ -905,7 +904,7 @@
         lax.fori_loop(
             share(index), share(index + 1), own_stage, 0
         )
-        if index % 3 == 1 and scans < rounds:
+        if index in SCAN_AT and scans < rounds:
             scan_step()
     for index in range(max(near_chunks - 1 - lag, -1), far_chunks):
         take_far(index)

time: 33.6 us -> 33.6 us (level)
  no operation moved by 1% of the time
where the time goes in v7:
time: 33.6 us; the launch traced here: 33.5 us
  Pallas kernels  32.1 us (96%)
  between operations  1.41 us (4%)
    pallas_call x1, Pallas kernels, fused_body(): pl.pallas_call(functools.partial(fused_kernel, dims), out_shape=(jax.Shap...  31.1 us
    pallas_call x1, Pallas kernels, body(): pl.pallas_call(put_kernel, out_shape=(jax.ShapeDtypeStruct(c_tiles.shape,...  0.99 us

profile of v7, /device:TPU:0, one launch (start us, length us, event | category | flops | bytes accessed | tf_op | source)
XLA Modules:
  0.0 33.5 jit_solution(11807139075341775670)
XLA Ops:
  0.6 0.0 copy-start.4
  0.6 0.0 copy-start.3
  0.7 0.0 copy-start.2
  0.7 0.0 copy-start
  0.7 0.0 copy-start.1
  0.7 31.1 %fused.1 = (bf16[32,128,128]{2,1,0:T(8,128)(2,1)S(1)}, s32[1,8]{1,0:T(1,128)S(1)}, s32[1,128]{1,0:T(1,128)}) custom-call(s32[8,8]{1,0:T(8,128)} %r_cols_hbm.1, s32[8,8]{1,0:T(8,128)} %c_cols_hbm.1, s32[1,8]{1,0:T(1,128)} %bitcast.71, s32[7,256]{1,0:T(8,128)} %bitcast.70, bf16[56,128,128]{2,1,0:T(8,128)(2,1)} %bitcast.31, bf16[64,128,128]{2,1,0:T(8,128)(2,1)} %bitcast.67), custom_call_target="tpu_custom_call" | custom-call | tf_op jit(solution)/shard_map/fused/pallas_call | solution.py:1049
  32.4 0.0 copy-done.4
  32.4 0.0 copy-done.3
  32.5 0.0 copy-done.2
  32.5 0.0 copy-done
  32.5 0.0 copy-done.1
  32.5 1.0 %put.1 = (bf16[8,4,128,128]{3,2,1,0:T(8,128)(2,1)}, s32[1,8]{1,0:T(1,128)}) custom-call(bf16[8,4,128,128]{3,2,1,0:T(8,128)(2,1)S(1)} %bitcast.69, s32[1,8]{1,0:T(1,128)S(1)} %get-tuple-element.183.offsets_ref), custom_call_target="tpu_custom_call" | custom-call | tf_op jit(solution)/shard_map/put/pallas_call | solution.py:1136
  (1 shorter events, 0.0 us)
Async XLA Ops:
  0.6 31.8 %copy-start.4 = (s32[8]{0:T(128)S(1)}, s32[8]{0:T(128)}, u32[]{:S(2)}) copy-start(s32[8]{0:T(128)} %param.30) | copy-start | bytes 100
  0.6 31.8 %copy-start.3 = (s32[8,8]{1,0:T(8,128)S(1)}, s32[8,8]{1,0:T(8,128)}, u32[]{:S(2)}) copy-start(s32[8,8]{1,0:T(8,128)} %c_cols_hbm.1) | copy-start | bytes 772
  0.7 31.8 %copy-start.2 = (s32[256,7]{0,1:T(8,128)S(1)}, s32[256,7]{0,1:T(8,128)}, u32[]{:S(2)}) copy-start(s32[256,7]{0,1:T(8,128)} %param.28) | copy-start | bytes 21508
  0.7 31.8 %copy-start = (bf16[8,7,128,128]{3,2,1,0:T(8,128)(2,1)S(1)}, bf16[8,7,128,128]{3,2,1,0:T(8,128)(2,1)}, u32[]{:S(2)}) copy-start(bf16[8,7,128,128]{3,2,1,0:T(8,128)(2,1)} %param.27) | copy-start | bytes 5505028
  0.7 31.8 %copy-start.1 = (s32[8,8]{1,0:T(8,128)S(1)}, s32[8,8]{1,0:T(8,128)}, u32[]{:S(2)}) copy-start(s32[8,8]{1,0:T(8,128)} %r_cols_hbm.1) | copy-start | bytes 772
